TPU v7x, 512 devices: a whole 4x8x8 slice. The times are simulated.
512 devices in a mesh: head: 8 (over y), leaf: 64 (over z, x, core).
Axes of the slice: x: 4, y: 8, z: 8, core: 2. Of those that a mesh axis runs over, the one named last changes fastest.
Arguments:
- queries: bfloat16 [128, 128, 8192], P('leaf', None, 'head'), may hold values from -6 to 6
- keys: bfloat16 [128, 128, 1024], P('leaf', 'head'), may hold values from -6 to 6
- values: bfloat16 [128, 128, 1024], P('leaf', 'head'), may hold values from -6 to 6
- output_gradient: bfloat16 [128, 128, 8192], P('leaf', None, 'head'), may hold values from -6 to 6
- parents: int32 [128], P('leaf'), may hold values from -1 to 127, as said below
Outputs:
- grad_queries: bfloat16 [128, 128, 8192], P('leaf', None, 'head')
- key_gradient: bfloat16 [128, 128, 1024], P('leaf', 'head')
- value_gradient: bfloat16 [128, 128, 1024], P('leaf', 'head')
Inputs may be any that keep to these rules, and one draw needn't show every extreme that they name: `parents`: block b is in tree b % 2 and its parent is in the same tree. In the tree of even blocks the parent lies below b and only block 0 is a root; in the tree of odd blocks the parent lies above b and only block 127 is a root. Every block has at most 14 ancestors, and some block has exactly 14.
All inputs are finite; a program needn't handle non-finite values.
Results may differ from a plain program's by a relative error of at most 0.012.
Values may be sent and summed in bfloat16 or wider, within the bound.
A program may use at most 64 MiB of HBM per device.

v0:
```python
import jax
import jax.numpy as jnp
from jax import lax
from jax.sharding import PartitionSpec as P

QUERY_HEAD_COUNT = 64
KEY_VALUE_HEADS = 8
HEAD_DIM = 128


masked_score = -1e30


def from_everyone(x, axis):
    copies = jnp.broadcast_to(x, (lax.axis_size(axis), *x.shape))
    return lax.all_to_all(copies, axis, split_axis=0, concat_axis=0, tiled=True)


def joined_along(pieces, dim):
    dims = list(pieces.shape[1:])
    dims[dim] *= pieces.shape[0]
    return jnp.moveaxis(pieces, 0, dim).reshape(dims)


def gathered_copies(x, axis, dim):
    pieces = from_everyone(x, axis)
    return joined_along(pieces, dim)


def in_one_piece(arrays, axis, split_dim, concat_dim, along):
    widths = [a.shape[along] for a in arrays]
    both = jnp.concatenate(arrays, axis=along)
    out = lax.all_to_all(both, axis, split_axis=split_dim, concat_axis=concat_dim, tiled=True)
    return tuple(jnp.split(out, [sum(widths[:k]) for k in range(1, len(widths))], axis=along))


def follow_links(parent_table, chain_len):

    def extend(link_no, carry_in):
        current, ancestry = carry_in
        ancestry = ancestry.at[:, link_no].set(current)
        upward = jnp.where(current >= 0, parent_table[jnp.maximum(current, 0)], -1)
        return (upward, ancestry)

    start = jnp.full((parent_table.shape[0], chain_len), -1, jnp.int32)
    return lax.fori_loop(0, chain_len, extend, (parent_table, start))[1]


def pick_rows(paired, need_left, need_right):
    left_tile = paired[0][None]
    right_tile = paired[1][None]
    array_shape = (need_left.shape[0],) + (1,) * (paired.ndim - 1)
    return jnp.where(
        need_left.reshape(array_shape),
        left_tile,
        jnp.where(need_right.reshape(array_shape), right_tile, jnp.zeros_like(left_tile)),
    )


def attend_block(
    query_rows, grad_rows, self_keys, self_values, chain_row, incoming, back_keys, back_values
):
    row_count = query_rows.shape[0]
    groups = self_keys.shape[1] // HEAD_DIM
    heads_per_group = QUERY_HEAD_COUNT // KEY_VALUE_HEADS
    softmax_scale = HEAD_DIM ** (-0.5)
    query_heads = query_rows.reshape(row_count, groups, heads_per_group, HEAD_DIM)
    grad_heads = grad_rows.reshape(row_count, groups, heads_per_group, HEAD_DIM)
    causal = lax.broadcasted_iota(jnp.int32, (row_count, row_count), 0) >= lax.broadcasted_iota(
        jnp.int32, (row_count, row_count), 1
    )

    def scores_of(block_keys):
        return (
            jnp.einsum(
                "igrd,jgd->grij",
                query_heads,
                block_keys.reshape(-1, groups, HEAD_DIM),
                preferred_element_type=jnp.float32,
            )
            * softmax_scale
        )

    def slopes_of(block_values):
        return jnp.einsum(
            "igrd,jgd->grij",
            grad_heads,
            block_values.reshape(-1, groups, HEAD_DIM),
            preferred_element_type=jnp.float32,
        )

    def fetch_tile(anc_block):
        tile = lax.dynamic_index_in_dim(incoming, anc_block // 2, 0, keepdims=False)
        return (tile[0], tile[1])

    scores = jnp.where(causal, scores_of(self_keys), masked_score)
    row_peak = jnp.max(scores, -1)
    shifted = jnp.exp(scores - row_peak[..., None])
    row_total = jnp.sum(shifted, -1)
    weighted = jnp.sum(shifted * slopes_of(self_values), -1)

    def first_sweep(link_no, carry_in):
        anc_block = chain_row[link_no]

        def first_active(status):
            old_peak, old_total, old_weighted = status
            block_keys, block_values = fetch_tile(anc_block)
            fresh = scores_of(block_keys)
            new_peak = jnp.maximum(old_peak, jnp.max(fresh, -1))
            factor = jnp.exp(old_peak - new_peak)
            shifted_here = jnp.exp(fresh - new_peak[..., None])
            return (
                new_peak,
                old_total * factor + jnp.sum(shifted_here, -1),
                old_weighted * factor + jnp.sum(shifted_here * slopes_of(block_values), -1),
            )

        return lax.cond(anc_block >= 0, first_active, lambda status: status, carry_in)

    row_peak, row_total, weighted = lax.fori_loop(
        0, chain_row.shape[0], first_sweep, (row_peak, row_total, weighted)
    )
    row_level = row_peak + jnp.log(row_total)
    row_mean = weighted / row_total

    def partials(block_keys, block_values, mask_on):
        fresh = scores_of(block_keys)
        if mask_on:
            fresh = jnp.where(causal, fresh, masked_score)
        weights = jnp.exp(fresh - row_level[..., None])
        dscore = (weights * (slopes_of(block_values) - row_mean[..., None])).astype(jnp.bfloat16)
        rounded = weights.astype(jnp.bfloat16)
        query_part = jnp.einsum(
            "grij,jgd->igrd",
            dscore,
            block_keys.reshape(-1, groups, HEAD_DIM),
            preferred_element_type=jnp.float32,
        )
        key_portion = (
            jnp.einsum("grij,igrd->jgd", dscore, query_heads, preferred_element_type=jnp.float32)
            * softmax_scale
        )
        value_portion = jnp.einsum(
            "grij,igrd->jgd", rounded, grad_heads, preferred_element_type=jnp.float32
        )
        return (
            query_part,
            key_portion.reshape(row_count, -1),
            value_portion.reshape(row_count, -1),
        )

    query_acc, key_self, value_self = partials(self_keys, self_values, True)

    def second(link_no, carry_in):
        anc_block = chain_row[link_no]

        def second_active(status):
            query_sum, keys_out, values_out = status
            block_keys, block_values = fetch_tile(anc_block)
            query_part, key_portion, value_portion = partials(block_keys, block_values, False)
            source = anc_block // 2
            keys_out = lax.dynamic_update_index_in_dim(
                keys_out,
                lax.dynamic_index_in_dim(keys_out, source, 0, keepdims=False) + key_portion,
                source,
                0,
            )
            values_out = lax.dynamic_update_index_in_dim(
                values_out,
                lax.dynamic_index_in_dim(values_out, source, 0, keepdims=False) + value_portion,
                source,
                0,
            )
            return (query_sum + query_part, keys_out, values_out)

        return lax.cond(anc_block >= 0, second_active, lambda status: status, carry_in)

    query_acc, back_keys, back_values = lax.fori_loop(
        0, chain_row.shape[0], second, (query_acc, back_keys, back_values)
    )
    query_grad = (query_acc * softmax_scale).astype(jnp.bfloat16).reshape(row_count, -1)
    return (query_grad, key_self, value_self, back_keys, back_values)


def body(queries, keys, values, output_gradient, parents):
    leaf_count = lax.axis_size("leaf")
    leaf_rank = lax.axis_index("leaf")
    chain_len = leaf_count // 4 - 2
    all_parents = gathered_copies(parents, "leaf", 0)
    ancestry = follow_links(all_parents, chain_len)
    need_left = jnp.any(ancestry[0::2] == 2 * leaf_rank, axis=1)
    need_right = jnp.any(ancestry[1::2] == 2 * leaf_rank + 1, axis=1)
    group_keys, group_values = in_one_piece((keys, values), "head", 2, 1, 0)
    outgoing = pick_rows(jnp.stack([group_keys, group_values], 1), need_left, need_right)
    incoming = lax.all_to_all(outgoing, "leaf", split_axis=0, concat_axis=0, tiled=True)
    kv_width = group_keys.shape[2]
    back_keys = jnp.zeros((leaf_count, group_keys.shape[1], kv_width), jnp.float32)
    back_values = jnp.zeros((leaf_count, group_keys.shape[1], kv_width), jnp.float32)
    query_grads = []
    key_selfs = []
    value_selfs = []
    for tree_no in range(2):
        chain_row = lax.dynamic_index_in_dim(ancestry, 2 * leaf_rank + tree_no, 0, keepdims=False)
        query_grad, key_self, value_self, back_keys, back_values = attend_block(
            queries[tree_no],
            output_gradient[tree_no],
            group_keys[tree_no],
            group_values[tree_no],
            chain_row,
            incoming,
            back_keys,
            back_values,
        )
        query_grads.append(query_grad)
        key_selfs.append(key_self)
        value_selfs.append(value_self)
    returned_keys, returned_values = tuple(
        (
            part.astype(jnp.float32)
            for part in in_one_piece(
                (back_keys.astype(jnp.bfloat16), back_values.astype(jnp.bfloat16)), "leaf", 0, 0, 1
            )
        )
    )
    mask_left = need_left[:, None, None]
    mask_right = need_right[:, None, None]
    key_left = key_selfs[0] + jnp.sum(jnp.where(mask_left, returned_keys, 0.0), 0)
    key_right = key_selfs[1] + jnp.sum(jnp.where(mask_right, returned_keys, 0.0), 0)
    value_left = value_selfs[0] + jnp.sum(jnp.where(mask_left, returned_values, 0.0), 0)
    value_right = value_selfs[1] + jnp.sum(jnp.where(mask_right, returned_values, 0.0), 0)
    local_keys = jnp.stack([key_left, key_right]).astype(jnp.bfloat16)
    local_values = jnp.stack([value_left, value_right]).astype(jnp.bfloat16)
    key_gradient, value_gradient = in_one_piece((local_keys, local_values), "head", 1, 2, 0)
    return (jnp.stack(query_grads), key_gradient, value_gradient)


def solution(mesh):
    in_specs = (
        P("leaf", None, "head"),
        P("leaf", "head", None),
        P("leaf", "head", None),
        P("leaf", None, "head"),
        P("leaf"),
    )
    out_specs = (P("leaf", None, "head"), P("leaf", "head", None), P("leaf", "head", None))
    return jax.shard_map(body, mesh=mesh, in_specs=in_specs, out_specs=out_specs, check_vma=False)
```

profile of v0, /device:TPU:6, one launch (start us, length us, event | category | flops | bytes accessed | tf_op | source)
XLA Modules:
  0.0 757.3 jit_solution(10918819054759962454)
XLA Ops:
  1.9 13.8 %all-to-all-start.1 = ((s32[64,1,2]{2,1,0:T(1,128)}), s32[64,1,2]{2,1,0:T(1,128)S(1)}, u32[]{:S(2)}, u32[]{:S(2)}) async-start(s32[64,1,2]{2,1,0:T(1,128)} %broadcast_in_dim.130), calls=%async_computation.1 | async-start | bytes 65536 | tf_op jit(solution)/shard_map/all_to_all | solution.py:16
  32.1 37.7 %while.84 = (s32[]{:T(128)}, s32[128]{0:T(128)S(1)}, s32[128,14]{0,1:T(8,128)S(1)}, s32[128]{0:T(128)S(1)}, s32[]{:T(128)}, /*index=5*/s32[1]{0:T(128)}, s32[]{:T(128)}) while((s32[]{:T(128)}, s32[128]{0:T(128)S(1)}, s32[128,14]{0,1:T(8,128)S(1)}, s32[128]{0:T(128)S(1)}, s32[]{:T(128)}, /*index=5*/s32[1]{0:T(128)}, s32[]{:T(128)}) %tuple.222), condition=%wide.region_5.6_spmd, body=%wide.region_3.0_spmd.sunk | while | flops 1549 | bytes 11359 | solution.py:46
  85.8 91.8 %all-to-all-done.2 = bf16[64,2,128,128]{3,2,1,0:T(8,128)(2,1)} async-done(((bf16[64,2,128,128]{3,2,1,0:T(8,128)(2,1)}), bf16[64,2,128,128]{3,2,1,0:T(8,128)(2,1)}, u32[]{:S(2)}, u32[]{:S(2)}) %all-to-all-start.2) | async-done | bytes 4194336 | tf_op jit(solution)/shard_map/all_to_all | solution.py:195
  177.6 43.0 %while.85 = (s32[]{:T(128)}, f32[1,8,128]{2,1,0:T(8,128)S(1)}, f32[1,8,128]{2,1,0:T(8,128)S(1)}, f32[1,8,128]{2,1,0:T(8,128)S(1)}, s32[14]{0:T(128)S(1)}, /*inde...) while((s32[]{:T(128)}, f32[1,8,128]{2,1,0:T(8,128)S(1)}, ...), condition=%wide.region_14.15_spmd, body=%wide.region_8.14_spmd.sunk | while | flops 68029456 | bytes 2236863 | solution.py:120
  227.0 68.6 %while.86 = (s32[]{:T(128)}, f32[128,1,8,128]{0,3,2,1:T(8,128)S(1)}, f32[64,128,128]{2,1,0:T(8,128)}, f32[64,128,128]{2,1,0:T(8,128)}, s32[14]{0:T(128)S(1)}, /*...) while((s32[]{:T(128)}, ...), condition=%wide.region_18.19_spmd, body=%wide.region_15.18_spmd.sunk | while | flops 168738832 | bytes 4825579 | solution.py:178
  277.5 8.7 %conditional.9 = ((f32[128,1,8,128]{0,3,2,1:T(8,128)S(1)}, f32[64,128,128]{2,1,0:T(8,128)}, f32[64,128,128]{2,1,0:T(8,128)})) conditional(s32[]{:T(128)} %convert_element_type.129, (f32[128,1,8,128]{0,3,2,1:T(8,128)S(1)}, f32[64,128,128]{2,1,0:T(8,128)}, f32[64,128,128]{2,1,0:T(8,128)}) %tuple.206, (s32[]{:T(128)}, ...), branch_computations={%region_16.16_spmd, %region_17.17_spmd} | conditional | flops 168738832 | bytes 4825340 | solution.py:176
  295.6 79.1 %while.87 = (s32[]{:T(128)}, f32[1,8,128]{2,1,0:T(8,128)S(1)}, f32[1,8,128]{2,1,0:T(8,128)S(1)}, f32[1,8,128]{2,1,0:T(8,128)S(1)}, s32[14]{0:T(128)S(1)}, /*inde...) while((s32[]{:T(128)}, f32[1,8,128]{2,1,0:T(8,128)S(1)}, ...), condition=%wide.region_28.29_spmd, body=%wide.region_22.28_spmd.sunk | while | flops 68029456 | bytes 2236863 | solution.py:120
  376.6 143.9 %while.88 = (s32[]{:T(128)}, f32[128,1,8,128]{0,3,2,1:T(8,128)S(1)}, f32[64,128,128]{2,1,0:T(8,128)}, f32[64,128,128]{2,1,0:T(8,128)}, s32[14]{0:T(128)S(1)}, /*...) while((s32[]{:T(128)}, ...), condition=%wide.region_32.33_spmd, body=%wide.region_29.32_spmd.sunk | while | flops 168738832 | bytes 4825579 | solution.py:178
  377.9 9.0 %conditional.11 = ((f32[128,1,8,128]{0,3,2,1:T(8,128)S(1)}, f32[64,128,128]{2,1,0:T(8,128)}, f32[64,128,128]{2,1,0:T(8,128)})) conditional(s32[]{:T(128)} %convert_element_type.131, (f32[128,1,8,128]{0,3,2,1:T(8,128)S(1)}, f32[64,128,128]{2,1,0:T(8,128)}, f32[64,128,128]{2,1,0:T(8,128)}) %tuple.212, (s32[]{:T(128)}, ...), branch_computations={%region_30.30_spmd, %region_31.31_spmd} | conditional | flops 168738832 | bytes 4825340 | solution.py:176
  388.1 9.0 %conditional.11 = ((f32[128,1,8,128]{0,3,2,1:T(8,128)S(1)}, f32[64,128,128]{2,1,0:T(8,128)}, f32[64,128,128]{2,1,0:T(8,128)})) conditional(s32[]{:T(128)} %convert_element_type.131, (f32[128,1,8,128]{0,3,2,1:T(8,128)S(1)}, f32[64,128,128]{2,1,0:T(8,128)}, f32[64,128,128]{2,1,0:T(8,128)}) %tuple.212, (s32[]{:T(128)}, ...), branch_computations={%region_30.30_spmd, %region_31.31_spmd} | conditional | flops 168738832 | bytes 4825340 | solution.py:176
  398.4 9.0 %conditional.11 = ((f32[128,1,8,128]{0,3,2,1:T(8,128)S(1)}, f32[64,128,128]{2,1,0:T(8,128)}, f32[64,128,128]{2,1,0:T(8,128)})) conditional(s32[]{:T(128)} %convert_element_type.131, (f32[128,1,8,128]{0,3,2,1:T(8,128)S(1)}, f32[64,128,128]{2,1,0:T(8,128)}, f32[64,128,128]{2,1,0:T(8,128)}) %tuple.212, (s32[]{:T(128)}, ...), branch_computations={%region_30.30_spmd, %region_31.31_spmd} | conditional | flops 168738832 | bytes 4825340 | solution.py:176
  408.7 9.0 %conditional.11 = ((f32[128,1,8,128]{0,3,2,1:T(8,128)S(1)}, f32[64,128,128]{2,1,0:T(8,128)}, f32[64,128,128]{2,1,0:T(8,128)})) conditional(s32[]{:T(128)} %convert_element_type.131, (f32[128,1,8,128]{0,3,2,1:T(8,128)S(1)}, f32[64,128,128]{2,1,0:T(8,128)}, f32[64,128,128]{2,1,0:T(8,128)}) %tuple.212, (s32[]{:T(128)}, ...), branch_computations={%region_30.30_spmd, %region_31.31_spmd} | conditional | flops 168738832 | bytes 4825340 | solution.py:176
  419.0 9.0 %conditional.11 = ((f32[128,1,8,128]{0,3,2,1:T(8,128)S(1)}, f32[64,128,128]{2,1,0:T(8,128)}, f32[64,128,128]{2,1,0:T(8,128)})) conditional(s32[]{:T(128)} %convert_element_type.131, (f32[128,1,8,128]{0,3,2,1:T(8,128)S(1)}, f32[64,128,128]{2,1,0:T(8,128)}, f32[64,128,128]{2,1,0:T(8,128)}) %tuple.212, (s32[]{:T(128)}, ...), branch_computations={%region_30.30_spmd, %region_31.31_spmd} | conditional | flops 168738832 | bytes 4825340 | solution.py:176
  429.3 9.0 %conditional.11 = ((f32[128,1,8,128]{0,3,2,1:T(8,128)S(1)}, f32[64,128,128]{2,1,0:T(8,128)}, f32[64,128,128]{2,1,0:T(8,128)})) conditional(s32[]{:T(128)} %convert_element_type.131, (f32[128,1,8,128]{0,3,2,1:T(8,128)S(1)}, f32[64,128,128]{2,1,0:T(8,128)}, f32[64,128,128]{2,1,0:T(8,128)}) %tuple.212, (s32[]{:T(128)}, ...), branch_computations={%region_30.30_spmd, %region_31.31_spmd} | conditional | flops 168738832 | bytes 4825340 | solution.py:176
  439.5 9.0 %conditional.11 = ((f32[128,1,8,128]{0,3,2,1:T(8,128)S(1)}, f32[64,128,128]{2,1,0:T(8,128)}, f32[64,128,128]{2,1,0:T(8,128)})) conditional(s32[]{:T(128)} %convert_element_type.131, (f32[128,1,8,128]{0,3,2,1:T(8,128)S(1)}, f32[64,128,128]{2,1,0:T(8,128)}, f32[64,128,128]{2,1,0:T(8,128)}) %tuple.212, (s32[]{:T(128)}, ...), branch_computations={%region_30.30_spmd, %region_31.31_spmd} | conditional | flops 168738832 | bytes 4825340 | solution.py:176
  449.8 9.0 %conditional.11 = ((f32[128,1,8,128]{0,3,2,1:T(8,128)S(1)}, f32[64,128,128]{2,1,0:T(8,128)}, f32[64,128,128]{2,1,0:T(8,128)})) conditional(s32[]{:T(128)} %convert_element_type.131, (f32[128,1,8,128]{0,3,2,1:T(8,128)S(1)}, f32[64,128,128]{2,1,0:T(8,128)}, f32[64,128,128]{2,1,0:T(8,128)}) %tuple.212, (s32[]{:T(128)}, ...), branch_computations={%region_30.30_spmd, %region_31.31_spmd} | conditional | flops 168738832 | bytes 4825340 | solution.py:176
  460.1 9.0 %conditional.11 = ((f32[128,1,8,128]{0,3,2,1:T(8,128)S(1)}, f32[64,128,128]{2,1,0:T(8,128)}, f32[64,128,128]{2,1,0:T(8,128)})) conditional(s32[]{:T(128)} %convert_element_type.131, (f32[128,1,8,128]{0,3,2,1:T(8,128)S(1)}, f32[64,128,128]{2,1,0:T(8,128)}, f32[64,128,128]{2,1,0:T(8,128)}) %tuple.212, (s32[]{:T(128)}, ...), branch_computations={%region_30.30_spmd, %region_31.31_spmd} | conditional | flops 168738832 | bytes 4825340 | solution.py:176
  470.4 9.0 %conditional.11 = ((f32[128,1,8,128]{0,3,2,1:T(8,128)S(1)}, f32[64,128,128]{2,1,0:T(8,128)}, f32[64,128,128]{2,1,0:T(8,128)})) conditional(s32[]{:T(128)} %convert_element_type.131, (f32[128,1,8,128]{0,3,2,1:T(8,128)S(1)}, f32[64,128,128]{2,1,0:T(8,128)}, f32[64,128,128]{2,1,0:T(8,128)}) %tuple.212, (s32[]{:T(128)}, ...), branch_computations={%region_30.30_spmd, %region_31.31_spmd} | conditional | flops 168738832 | bytes 4825340 | solution.py:176
  480.7 9.0 %conditional.11 = ((f32[128,1,8,128]{0,3,2,1:T(8,128)S(1)}, f32[64,128,128]{2,1,0:T(8,128)}, f32[64,128,128]{2,1,0:T(8,128)})) conditional(s32[]{:T(128)} %convert_element_type.131, (f32[128,1,8,128]{0,3,2,1:T(8,128)S(1)}, f32[64,128,128]{2,1,0:T(8,128)}, f32[64,128,128]{2,1,0:T(8,128)}) %tuple.212, (s32[]{:T(128)}, ...), branch_computations={%region_30.30_spmd, %region_31.31_spmd} | conditional | flops 168738832 | bytes 4825340 | solution.py:176
  491.0 9.0 %conditional.11 = ((f32[128,1,8,128]{0,3,2,1:T(8,128)S(1)}, f32[64,128,128]{2,1,0:T(8,128)}, f32[64,128,128]{2,1,0:T(8,128)})) conditional(s32[]{:T(128)} %convert_element_type.131, (f32[128,1,8,128]{0,3,2,1:T(8,128)S(1)}, f32[64,128,128]{2,1,0:T(8,128)}, f32[64,128,128]{2,1,0:T(8,128)}) %tuple.212, (s32[]{:T(128)}, ...), branch_computations={%region_30.30_spmd, %region_31.31_spmd} | conditional | flops 168738832 | bytes 4825340 | solution.py:176
  501.2 9.0 %conditional.11 = ((f32[128,1,8,128]{0,3,2,1:T(8,128)S(1)}, f32[64,128,128]{2,1,0:T(8,128)}, f32[64,128,128]{2,1,0:T(8,128)})) conditional(s32[]{:T(128)} %convert_element_type.131, (f32[128,1,8,128]{0,3,2,1:T(8,128)S(1)}, f32[64,128,128]{2,1,0:T(8,128)}, f32[64,128,128]{2,1,0:T(8,128)}) %tuple.212, (s32[]{:T(128)}, ...), branch_computations={%region_30.30_spmd, %region_31.31_spmd} | conditional | flops 168738832 | bytes 4825340 | solution.py:176
  511.5 9.0 %conditional.11 = ((f32[128,1,8,128]{0,3,2,1:T(8,128)S(1)}, f32[64,128,128]{2,1,0:T(8,128)}, f32[64,128,128]{2,1,0:T(8,128)})) conditional(s32[]{:T(128)} %convert_element_type.131, (f32[128,1,8,128]{0,3,2,1:T(8,128)S(1)}, f32[64,128,128]{2,1,0:T(8,128)}, f32[64,128,128]{2,1,0:T(8,128)}) %tuple.212, (s32[]{:T(128)}, ...), branch_computations={%region_30.30_spmd, %region_31.31_spmd} | conditional | flops 168738832 | bytes 4825340 | solution.py:176
  526.9 110.3 %all-to-all-start.3 = ((bf16[64,256,128]{2,1,0:T(8,128)(2,1)}), bf16[64,256,128]{2,1,0:T(8,128)(2,1)}, u32[]{:S(2)}, u32[]{:S(2)}) async-start(bf16[64,256,128]{2,1,0:T(8,128)(2,1)} %pad_maximum_fusion), calls=%async_computation.3 | async-start | bytes 8388608 | tf_op jit(solution)/shard_map/all_to_all | solution.py:33
  638.0 95.3 %all-to-all-done.3 = bf16[64,256,128]{2,1,0:T(8,128)(2,1)} async-done(((bf16[64,256,128]{2,1,0:T(8,128)(2,1)}), bf16[64,256,128]{2,1,0:T(8,128)(2,1)}, u32[]{:S(2)}, u32[]{:S(2)}) %all-to-all-start.3) | async-done | bytes 4194336 | tf_op jit(solution)/shard_map/all_to_all | solution.py:33
  (509 shorter events, 444.3 us)
Async XLA Ops:
  1.9 21.7 %all-to-all-start.1 = ((s32[64,1,2]{2,1,0:T(1,128)}), s32[64,1,2]{2,1,0:T(1,128)S(1)}, u32[]{:S(2)}, u32[]{:S(2)}) async-start(s32[64,1,2]{2,1,0:T(1,128)} %broadcast_in_dim.130), calls=%async_computation.1 | async-start | bytes 65536 | tf_op jit(solution)/shard_map/all_to_all | solution.py:16
  23.6 46.7 %all-to-all-start = ((bf16[8,2,4096]{2,1,0:T(2,128)(2,1)}), bf16[8,2,4096]{2,1,0:T(2,128)(2,1)S(1)}, u32[]{:S(2)}, u32[]{:S(2)}) async-start(bf16[8,2,4096]{2,1,0:T(2,128)(2,1)} %reshape.476), calls=%async_computation | async-start | bytes 262144 | tf_op jit(solution)/shard_map/all_to_all | solution.py:33
  74.0 7.4 copy-start.11
  74.0 7.6 %copy-start.12 = (bf16[2,128,1024]{2,1,0:T(8,128)(2,1)S(1)}, bf16[2,128,1024]{2,1,0:T(8,128)(2,1)}, u32[]{:S(2)}) copy-start(bf16[2,128,1024]{2,1,0:T(8,128)(2,1)} %param.28) | copy-start | bytes 1572868
  74.0 103.6 %all-to-all-start.2 = ((bf16[64,2,128,128]{3,2,1,0:T(8,128)(2,1)}), bf16[64,2,128,128]{3,2,1,0:T(8,128)(2,1)}, u32[]{:S(2)}, u32[]{:S(2)}) async-start(bf16[64,2,128,128]{3,2,1,0:T(8,128)(2,1)} %select_select_fusion), calls=%async_computation.2 | async-start | bytes 8388608 | tf_op jit(solution)/shard_map/all_to_all | solution.py:195
  81.9 95.7 %copy-start.3 = (bf16[1,128,1024]{1,2,0:T(8,128)(2,1)}, bf16[1,128,1024]{1,2,0:T(8,128)(2,1)S(1)}, u32[]{:S(2)}) copy-start(bf16[1,128,1024]{1,2,0:T(8,128)(2,1)S(1)} %copy.156) | copy-start | bytes 786436
  82.4 95.2 %copy-start.1 = (bf16[1,128,1024]{1,2,0:T(8,128)(2,1)}, bf16[1,128,1024]{1,2,0:T(8,128)(2,1)S(1)}, u32[]{:S(2)}) copy-start(bf16[1,128,1024]{1,2,0:T(8,128)(2,1)S(1)} %copy.157) | copy-start | bytes 786436
  82.6 95.0 %copy-start.5 = (bf16[1,128,1024]{1,2,0:T(8,128)(2,1)}, bf16[1,128,1024]{1,2,0:T(8,128)(2,1)S(1)}, u32[]{:S(2)}) copy-start(bf16[1,128,1024]{1,2,0:T(8,128)(2,1)S(1)} %copy.158) | copy-start | bytes 786436
  221.8 5.2 copy-start.7
  375.9 0.7 copy-start.9
  520.6 3.5 copy-start
  526.9 206.4 %all-to-all-start.3 = ((bf16[64,256,128]{2,1,0:T(8,128)(2,1)}), bf16[64,256,128]{2,1,0:T(8,128)(2,1)}, u32[]{:S(2)}, u32[]{:S(2)}) async-start(bf16[64,256,128]{2,1,0:T(8,128)(2,1)} %pad_maximum_fusion), calls=%async_computation.3 | async-start | bytes 8388608 | tf_op jit(solution)/shard_map/all_to_all | solution.py:33
  637.2 99.6 %copy-start.8 = (bf16[8,128,128]{1,2,0:T(8,128)(2,1)S(1)}, bf16[8,128,128]{1,2,0:T(8,128)(2,1)}, u32[]{:S(2)}) copy-start(bf16[8,128,128]{1,2,0:T(8,128)(2,1)} %copy-done.7) | copy-start | bytes 786436
  637.2 99.9 %copy-start.2 = (bf16[1,128,1024]{1,2,0:T(8,128)(2,1)S(1)}, bf16[1,128,1024]{1,2,0:T(8,128)(2,1)}, u32[]{:S(2)}) copy-start(bf16[1,128,1024]{1,2,0:T(8,128)(2,1)} %copy-done.1) | copy-start | bytes 786436
  637.2 101.0 %copy-start.4 = (bf16[1,128,1024]{1,2,0:T(8,128)(2,1)S(1)}, bf16[1,128,1024]{1,2,0:T(8,128)(2,1)}, u32[]{:S(2)}) copy-start(bf16[1,128,1024]{1,2,0:T(8,128)(2,1)} %copy-done.3) | copy-start | bytes 786436
  637.2 101.3 %copy-start.6 = (bf16[1,128,1024]{1,2,0:T(8,128)(2,1)S(1)}, bf16[1,128,1024]{1,2,0:T(8,128)(2,1)}, u32[]{:S(2)}) copy-start(bf16[1,128,1024]{1,2,0:T(8,128)(2,1)} %copy-done.5) | copy-start | bytes 786436
  638.0 108.8 %copy-start.10 = (bf16[128,1,8,128]{0,3,2,1:T(8,128)(2,1)S(1)}, bf16[128,1,8,128]{0,3,2,1:T(8,128)(2,1)}, u32[]{:S(2)}) copy-start(bf16[128,1,8,128]{0,3,2,1:T(8,128)(2,1)} %multiply_convert_fusion) | copy-start | bytes 786436
  739.5 16.3 %all-to-all-start.4 = ((bf16[4,128,128]{2,0,1:T(4,128)(2,1)}), bf16[4,128,128]{2,0,1:T(4,128)(2,1)S(1)}, u32[]{:S(2)}, u32[]{:S(2)}) async-start(bf16[4,128,128]{2,0,1:T(4,128)(2,1)} %copy.130), calls=%async_computation.4 | async-start | bytes 262144 | tf_op jit(solution)/shard_map/all_to_all | solution.py:33
where the time goes:
time: 773 us; the launch traced here: 757 us
  waiting for transfers between devices  200 us (26%)
  matrix products  172 us (22%)
  starting transfers between devices  146 us (19%)
  loops' own time  133 us (17%)
  local copies, waits for them, and re-layouts  66.6 us (9%)
  other arithmetic  38.5 us (5%)
    all_to_all x3, starting transfers between devices, in_one_piece(): lax.all_to_all(both, axis, split_axis=split_dim, concat_axis=concat_dim,...  125 us
    all_to_all x3, waiting for transfers between devices, in_one_piece(): lax.all_to_all(both, axis, split_axis=split_dim, concat_axis=concat_dim,...  103 us
    all_to_all x1, waiting for transfers between devices, body(): lax.all_to_all(outgoing, 'leaf', split_axis=0, concat_axis=0, tiled=True)  91.8 us
    another operation x28, loops' own time, second(): lax.cond(anc_block >= 0, second_active, lambda status: status, carry_in)  51.2 us
    another operation x28, loops' own time, first_sweep(): lax.cond(anc_block >= 0, first_active, lambda status: status, carry_in)  46.9 us
    dot_general x42, matrix products, slopes_of(): jnp.einsum('igrd,jgd->grij', grad_heads, block_values.reshape(-1, groups,...  42.2 us
    dot_general x42, matrix products, scores_of(): jnp.einsum('igrd,jgd->grij', query_heads, block_keys.reshape(-1, groups,...  40.3 us
    dot_general x22, matrix products, partials(): jnp.einsum('grij,igrd->jgd', dscore, query_heads, preferred_element_type=...  35.2 us
  transfers between devices with their start and end apart: 5, of which 4 were waited for; matrix products, arithmetic and copies ran while one was open for 6% of the time, Pallas kernels for 0%

commit v1 on v0

v1 whole, which is shorter than its diff:
```python
import functools

import jax
import jax.numpy as jnp
from jax import lax
from jax.experimental import pallas as pl
from jax.experimental.pallas import tpu as pltpu
from jax.sharding import PartitionSpec as P

QUERY_HEAD_COUNT = 64
KEY_VALUE_HEADS = 8
HEAD_DIM = 128
BLOCK_TOKENS = 128
MAX_ANCESTORS = 14
HEADS_PER_GROUP = QUERY_HEAD_COUNT // KEY_VALUE_HEADS
CHAIN = MAX_ANCESTORS + 1

X_CHIPS = 4
ROW = 2 * X_CHIPS
PARENT_ROWS = 16
KV_ROWS = 2 * BLOCK_TOKENS
TILE_ROWS = KV_ROWS + PARENT_ROWS
VMEM_LIMIT = 56 * 1024 * 1024
masked_score = -1e30
MESH = pl.DeviceIdType.MESH


class Place:
    def __init__(self, heads, leaves):
        self.heads, self.layers = heads, leaves // ROW
        self.y = lax.axis_index("head")
        self.leaf = lax.axis_index("leaf")
        self.z = self.leaf // ROW
        self.x = (self.leaf % ROW) // 2
        self.core = self.leaf % 2

    def column(self, step):
        return (self.x + step + X_CHIPS) % X_CHIPS

    def leaf_of(self, z, x, core):
        return z * ROW + x * 2 + core

    def along_x(self, step):
        return (self.y, self.leaf_of(self.z, self.column(step), self.core))

    def along_z(self, step):
        return (self.y, self.leaf_of(self.z + step, self.x, self.core))

    def sibling(self):
        return (self.y, self.leaf_of(self.z, self.x, 1 - self.core))

    def head_peer(self, step):
        return ((self.y + step) % self.heads, self.leaf)

    def greet(self):
        barrier = pltpu.get_barrier_semaphore()

        def signal(device):
            pl.semaphore_signal(barrier, inc=1, device_id=device, device_id_type=MESH)

        for step in range(1, self.heads):
            signal(self.head_peer(step))
        for step in range(1, X_CHIPS):
            signal(self.along_x(step))
        signal(self.sibling())

        @pl.when(self.z > 0)
        def _():
            signal(self.along_z(-1))

        @pl.when(self.z < self.layers - 1)
        def _():
            signal(self.along_z(1))

        inner = ((self.z > 0) & (self.z < self.layers - 1)).astype(jnp.int32)
        pl.semaphore_wait(barrier, self.heads - 1 + X_CHIPS - 1 + 1 + 1 + inner)


def remote(src, dst, send_sem, recv_sem, device):
    return pltpu.make_async_remote_copy(
        src_ref=src, dst_ref=dst, send_sem=send_sem, recv_sem=recv_sem,
        device_id=device, device_id_type=MESH,
    )


def gather_kernel(
    heads, leaves, keys, values, marks, own, buf,
    y_send, y_recv, z_send, z_recv, r_send, r_recv, x_send, x_recv, h_send, h_recv,
    d_send, d_recv, e_send, e_recv,
):
    at = Place(heads, leaves)
    layers, z, x, core = at.layers, at.z, at.x, at.core
    share = BLOCK_TOKENS // heads
    at.greet()

    def regroup(step):
        column = pl.ds(pl.multiple_of(((at.y + step) % heads) * HEAD_DIM, HEAD_DIM), HEAD_DIM)
        rows_k = pl.ds(pl.multiple_of(at.y * share, share), share)
        rows_v = pl.ds(pl.multiple_of(BLOCK_TOKENS + at.y * share, share), share)
        peer = at.head_peer(step)
        return (
            remote(keys.at[:, :, column], own.at[:, rows_k, :],
                   y_send.at[2 * step], y_recv.at[2 * step], peer),
            remote(values.at[:, :, column], own.at[:, rows_v, :],
                   y_send.at[2 * step + 1], y_recv.at[2 * step + 1], peer),
        )

    for step in range(1, heads):
        for copy in regroup(step):
            copy.start()
    mine = pl.ds(pl.multiple_of(at.y * HEAD_DIM, HEAD_DIM), HEAD_DIM)
    own[:, pl.ds(pl.multiple_of(at.y * share, share), share), :] = keys[:, :, mine]
    own[:, pl.ds(pl.multiple_of(BLOCK_TOKENS + at.y * share, share), share), :] = values[:, :, mine]
    own[:, KV_ROWS:, :] = marks[...]
    for step in range(1, heads):
        for copy in regroup(step):
            copy.wait_recv()

    def slot(zz, xx, cc):
        return buf.at[zz, xx, cc]

    up_send = z_send.at[layers]
    down_send = z_send.at[layers + 1]

    def first_up():
        return remote(own.at[0], slot(z, x, core), up_send, z_recv.at[z], at.along_z(1))

    def first_down():
        return remote(own.at[1], slot(z, x, core), down_send, z_recv.at[z], at.along_z(-1))

    pl.when(z < layers - 1)(lambda: first_up().start())
    pl.when(z > 0)(lambda: first_down().start())

    def row_copy(step):
        tree = (at.column(step) < x).astype(jnp.int32)
        return remote(own.at[tree], slot(z, x, core), r_send.at[step], r_recv.at[step],
                      at.along_x(step))

    for step in (1, 3, 2):
        row_copy(step).start()

    def twin_copy():
        return remote(own.at[core], slot(z, x, core), e_send.at[0], e_recv.at[0], at.sibling())

    twin_copy().start()

    def row_from(step):
        tile = slot(z, at.column(-step), core)
        return remote(tile, tile, e_send.at[step], e_recv.at[step], at.sibling())

    def z_arrival(source):
        tile = slot(source, x, core)
        return remote(tile, tile, z_send.at[source], z_recv.at[source], at.sibling())

    def z_next(source, step):
        tile = slot(source, x, core)
        return remote(tile, tile, z_send.at[source], z_recv.at[source], at.along_z(step))

    def x_copy(source, step):
        tile = slot(source, x, core)
        side = 0 if step > 0 else 1
        return remote(tile, tile, x_send.at[side, source], x_recv.at[side, source],
                      at.along_x(step))

    def x_half(source, step):
        side = 0 if step > 0 else 1
        rows = pl.ds(0, BLOCK_TOKENS) if step > 0 else pl.ds(BLOCK_TOKENS, TILE_ROWS - BLOCK_TOKENS)
        tile = buf.at[source, at.column(-step), core, rows]
        return remote(tile, tile, h_send.at[side, source], h_recv.at[side, source],
                      at.along_x(step))

    def twin_row(source):
        part = buf.at[source, :, core]
        return remote(part, part, d_send.at[source], d_recv.at[source], at.sibling())

    def both(step, action):
        if step < 1 or step > layers - 1:
            return
        pl.when(z - step >= 0)(lambda: action(z - step, 1))
        pl.when(z + step <= layers - 1)(lambda: action(z + step, -1))

    def arrive(source, way):
        z_arrival(source).wait_recv()
        more = (z < layers - 1) if way > 0 else (z > 0)
        pl.when(more)(lambda: z_next(source, way).start())
        x_copy(source, 1).start()
        x_copy(source, -1).start()

    def across(source, way):
        x_copy(source, 1).wait_recv()
        x_half(source, 1).start()
        x_copy(source, -1).wait_recv()
        x_half(source, -1).start()

    def share_row(source, way):
        x_half(source, 1).wait_recv()
        x_half(source, -1).wait_recv()
        twin_row(source).start()

    for step in range(1, layers + 2):
        both(step, arrive)
        if step == 1:
            for hop in (1, 3, 2):
                row_copy(hop).wait_recv()
                row_from(hop).start()
        both(step - 1, across)
        both(step - 2, share_row)

    twin_copy().wait_recv()
    for hop in (1, 3, 2):
        row_from(hop).wait_recv()
    for step in range(1, layers):
        both(step, lambda source, way: twin_row(source).wait_recv())

    for step in range(1, heads):
        for copy in regroup(step):
            copy.wait_send()
    pl.when(z < layers - 1)(lambda: first_up().wait_send())
    pl.when(z > 0)(lambda: first_down().wait_send())
    twin_copy().wait_send()
    for hop in (1, 3, 2):
        row_copy(hop).wait_send()
        row_from(hop).wait_send()

    def drain(source, way):
        more = (z < layers - 1) if way > 0 else (z > 0)
        pl.when(more)(lambda: z_next(source, way).wait_send())
        for step in (1, -1):
            x_copy(source, step).wait_send()
            x_half(source, step).wait_send()
        twin_row(source).wait_send()

    for step in range(1, layers):
        both(step, drain)


def gather_tiles(keys, values, marks, heads, leaves):
    layers = leaves // ROW
    dma = pltpu.SemaphoreType.DMA
    vmem = pl.BlockSpec(memory_space=pltpu.VMEM)
    return pl.pallas_call(
        functools.partial(gather_kernel, heads, leaves),
        out_shape=(
            jax.ShapeDtypeStruct((2, TILE_ROWS, HEAD_DIM), jnp.bfloat16),
            jax.ShapeDtypeStruct((layers, X_CHIPS, 2, TILE_ROWS, HEAD_DIM), jnp.bfloat16),
        ),
        in_specs=[vmem] * 3,
        out_specs=(vmem, vmem),
        scratch_shapes=[
            dma((2 * heads,)), dma((2 * heads,)),
            dma((layers + 2,)), dma((layers,)),
            dma((X_CHIPS,)), dma((X_CHIPS,)),
            dma((2, layers)), dma((2, layers)),
            dma((2, layers)), dma((2, layers)),
            dma((layers,)), dma((layers,)),
            dma((X_CHIPS,)), dma((X_CHIPS,)),
        ],
        compiler_params=pltpu.CompilerParams(
            collective_id=0, has_side_effects=True, vmem_limit_bytes=VMEM_LIMIT
        ),
        name="gather_tiles",
    )(keys, values, marks)


LANES = 2 * BLOCK_TOKENS
SPAN = CHAIN * BLOCK_TOKENS
PART = 3 * BLOCK_TOKENS
PARTS = SPAN // PART


def attend_kernel(
    table, first, queries, grads, own, buf, dq, selfs, back,
    kcat, vcat, kcat_t, q2, g2, s_scr, l_scr, p_all, d_all,
):
    softmax_scale = HEAD_DIM ** -0.5
    log2_scale = softmax_scale * 1.4426950408889634
    rows = HEADS_PER_GROUP * BLOCK_TOKENS
    nt = (((1,), (1,)), ((), ()))
    back[...] = jnp.zeros_like(back)

    def one_tree(tree, carry):
        kcat[:BLOCK_TOKENS] = own[tree, :BLOCK_TOKENS]
        vcat[:BLOCK_TOKENS] = own[tree, BLOCK_TOKENS:KV_ROWS]
        current = first[tree]
        alive, ranks = [], []
        for link in range(MAX_ANCESTORS):
            active = current >= 0
            rank = jnp.right_shift(jnp.maximum(current, 0), 1)
            place = slice((link + 1) * BLOCK_TOKENS, (link + 2) * BLOCK_TOKENS)

            @pl.when(active)
            def _():
                kcat[place] = buf[rank, :BLOCK_TOKENS]
                vcat[place] = buf[rank, BLOCK_TOKENS:KV_ROWS]

            @pl.when(jnp.logical_not(active))
            def _():
                kcat[place] = own[tree, :BLOCK_TOKENS]
                vcat[place] = own[tree, BLOCK_TOKENS:KV_ROWS]

            alive.append(active)
            ranks.append(rank)
            current = jnp.where(active, table[rank], -1)
        for link in range(CHAIN):
            place = slice(link * BLOCK_TOKENS, (link + 1) * BLOCK_TOKENS)
            kcat_t[:, place] = kcat[place].T
        for head in range(HEADS_PER_GROUP):
            place = slice(head * BLOCK_TOKENS, (head + 1) * BLOCK_TOKENS)
            q2[place] = queries[tree, :, place]
            g2[place] = grads[tree, :, place]

        key_pos = lax.broadcasted_iota(jnp.int32, (BLOCK_TOKENS, LANES), 0)
        row_pos = lax.broadcasted_iota(jnp.int32, (BLOCK_TOKENS, LANES), 1) % BLOCK_TOKENS
        causal = key_pos <= row_pos

        def head_pair(pair, carry):
            lanes = pl.ds(pl.multiple_of(pair * LANES, LANES), LANES)
            q_pair = q2[lanes]
            g_pair = g2[lanes]
            peak = None
            for part in range(PARTS):
                place = slice(part * PART, (part + 1) * PART)
                raw = lax.dot_general(kcat[place], q_pair, nt, preferred_element_type=jnp.float32)
                l_scr[place] = lax.dot_general(
                    vcat[place], g_pair, nt, preferred_element_type=jnp.float32
                )
                for block in range(PART // BLOCK_TOKENS):
                    link = part * (PART // BLOCK_TOKENS) + block
                    score = raw[block * BLOCK_TOKENS:(block + 1) * BLOCK_TOKENS] * log2_scale
                    if link == 0:
                        score = jnp.where(causal, score, masked_score)
                    else:
                        score = score + jnp.where(alive[link - 1], 0.0, masked_score)
                    s_scr[link * BLOCK_TOKENS:(link + 1) * BLOCK_TOKENS] = score
                    top = jnp.max(score.reshape(BLOCK_TOKENS // 8, 8, LANES), 0)
                    peak = top if peak is None else jnp.maximum(peak, top)
            peak = jnp.max(peak, 0, keepdims=True)
            total = jnp.zeros((8, LANES), jnp.float32)
            lean = jnp.zeros((8, LANES), jnp.float32)
            for link in range(CHAIN):
                place = slice(link * BLOCK_TOKENS, (link + 1) * BLOCK_TOKENS)
                shifted = jnp.exp2(s_scr[place] - peak)
                s_scr[place] = shifted
                total = total + jnp.sum(shifted.reshape(-1, 8, LANES), 0)
                lean = lean + jnp.sum((shifted * l_scr[place]).reshape(-1, 8, LANES), 0)
            inverse = 1.0 / jnp.sum(total, 0, keepdims=True)
            mean = jnp.sum(lean, 0, keepdims=True) * inverse
            query_part = jnp.zeros((HEAD_DIM, LANES), jnp.float32)
            for part in range(PARTS):
                place = slice(part * PART, (part + 1) * PART)
                weights = s_scr[place] * inverse
                dscore = (weights * (l_scr[place] - mean)).astype(jnp.bfloat16)
                p_all[place, lanes] = weights.astype(jnp.bfloat16)
                d_all[place, lanes] = dscore
                query_part = query_part + jnp.dot(
                    kcat_t[:, place], dscore, preferred_element_type=jnp.float32
                )
            query_part = (query_part * softmax_scale).T.astype(jnp.bfloat16)
            for half in range(2):
                column = pl.multiple_of(pair * LANES + half * HEAD_DIM, HEAD_DIM)
                dq[tree, :, pl.ds(column, HEAD_DIM)] = query_part[
                    half * BLOCK_TOKENS:(half + 1) * BLOCK_TOKENS
                ]
            return carry

        lax.fori_loop(0, rows // LANES, head_pair, 0)

        for part in range(PARTS):
            place = slice(part * PART, (part + 1) * PART)
            key_part = softmax_scale * jnp.dot(
                d_all[place], q2[...], preferred_element_type=jnp.float32
            )
            value_part = jnp.dot(p_all[place], g2[...], preferred_element_type=jnp.float32)
            for block in range(PART // BLOCK_TOKENS):
                link = part * (PART // BLOCK_TOKENS) + block
                here = slice(block * BLOCK_TOKENS, (block + 1) * BLOCK_TOKENS)
                if link == 0:
                    selfs[tree, :BLOCK_TOKENS] = key_part[here]
                    selfs[tree, BLOCK_TOKENS:] = value_part[here]
                else:

                    @pl.when(alive[link - 1])
                    def _():
                        back[ranks[link - 1], :BLOCK_TOKENS] = key_part[here].astype(jnp.bfloat16)
                        back[ranks[link - 1], BLOCK_TOKENS:] = value_part[here].astype(jnp.bfloat16)

        return carry

    lax.fori_loop(0, 2, one_tree, 0)


def attend(table, first, queries, grads, own, buf):
    leaves = buf.shape[0]
    rows = HEADS_PER_GROUP * BLOCK_TOKENS
    vmem = pl.BlockSpec(memory_space=pltpu.VMEM)
    smem = pl.BlockSpec(memory_space=pltpu.SMEM)
    bf16, f32 = jnp.bfloat16, jnp.float32
    return pl.pallas_call(
        attend_kernel,
        out_shape=(
            jax.ShapeDtypeStruct(queries.shape, bf16),
            jax.ShapeDtypeStruct((2, KV_ROWS, HEAD_DIM), f32),
            jax.ShapeDtypeStruct((leaves, KV_ROWS, HEAD_DIM), bf16),
        ),
        in_specs=[smem, smem, vmem, vmem, vmem, vmem],
        out_specs=(vmem, vmem, vmem),
        scratch_shapes=[
            pltpu.VMEM((SPAN, HEAD_DIM), bf16),
            pltpu.VMEM((SPAN, HEAD_DIM), bf16),
            pltpu.VMEM((HEAD_DIM, SPAN), bf16),
            pltpu.VMEM((rows, HEAD_DIM), bf16),
            pltpu.VMEM((rows, HEAD_DIM), bf16),
            pltpu.VMEM((SPAN, LANES), f32),
            pltpu.VMEM((SPAN, LANES), f32),
            pltpu.VMEM((SPAN, rows), bf16),
            pltpu.VMEM((SPAN, rows), bf16),
        ],
        compiler_params=pltpu.CompilerParams(vmem_limit_bytes=VMEM_LIMIT),
        cost_estimate=pl.CostEstimate(
            flops=10 * SPAN * rows * HEAD_DIM * 2, bytes_accessed=12 << 20,
            transcendentals=2 * SPAN * rows,
        ),
        name="attend",
    )(table, first, queries, grads, own, buf)


def scatter_kernel(
    heads, leaves, selfs, back, key_out, value_out,
    sums, d_in, e_in, x_in, h_in, r_in, z_in, total, final,
    y_send, y_recv, z_send, z_recv, r_send, r_recv, x_send, x_recv, h_send, h_recv,
    d_send, d_recv, e_send, e_recv,
):
    at = Place(heads, leaves)
    layers, z, x, core = at.layers, at.z, at.x, at.core
    share = BLOCK_TOKENS // heads
    f32, bf16 = jnp.float32, jnp.bfloat16
    at.greet()

    def both(step, action):
        if step < 1 or step > layers - 1:
            return
        pl.when(z - step >= 0)(lambda: action(z - step, 1))
        pl.when(z + step <= layers - 1)(lambda: action(z + step, -1))

    def twin_row(source):
        return remote(back.at[source, :, 1 - core], d_in.at[source], d_send.at[source],
                      d_recv.at[source], at.sibling())

    def twin_tile(step):
        column = at.column(step)
        return remote(back.at[z, column, 1 - core], e_in.at[column],
                      e_send.at[step], e_recv.at[step], at.sibling())

    for step in range(layers - 1, 0, -1):
        both(step, lambda source, way: twin_row(source).start())
    for step in range(X_CHIPS):
        twin_tile(step).start()

    keys_half = pl.ds(0, BLOCK_TOKENS)
    values_half = pl.ds(BLOCK_TOKENS, BLOCK_TOKENS)

    def x_half(source, step):
        side = 0 if step > 0 else 1
        rows = values_half if step > 0 else keys_half
        return remote(sums.at[source, at.column(2), rows], h_in.at[side, source],
                      h_send.at[side, source], h_recv.at[side, source], at.along_x(step))

    def x_copy(source, step):
        side = 0 if step > 0 else 1
        return remote(sums.at[source, at.column(step)], x_in.at[side, source],
                      x_send.at[side, source], x_recv.at[side, source], at.along_x(step))

    def z_next(source, way):
        place = source if way > 0 else jnp.where(source == z + 1, layers, source)
        return remote(sums.at[source, x], z_in.at[place], z_send.at[source], z_recv.at[place],
                      at.along_z(-way))

    def z_arrival(place):
        return remote(z_in.at[place], z_in.at[place], z_send.at[z], z_recv.at[place], at.sibling())

    def row_copy(step):
        return remote(sums.at[z, at.column(step)], r_in.at[step], r_send.at[step],
                      r_recv.at[step], at.along_x(step))

    def merge_twin(source, way):
        twin_row(source).wait_recv()
        for column in range(X_CHIPS):
            sums[source, column] = (
                back[source, column, core].astype(f32) + d_in[source, column].astype(f32)
            ).astype(bf16)
        x_half(source, 1).start()
        x_half(source, -1).start()

    def merge_half(source, way):
        x_half(source, 1).wait_recv()
        right = at.column(1)
        sums[source, right, values_half] = (
            sums[source, right, values_half].astype(f32) + h_in[0, source].astype(f32)
        ).astype(bf16)
        x_copy(source, 1).start()
        x_half(source, -1).wait_recv()
        left = at.column(-1)
        sums[source, left, keys_half] = (
            sums[source, left, keys_half].astype(f32) + h_in[1, source].astype(f32)
        ).astype(bf16)
        x_copy(source, -1).start()

    def merge_across(source, way):
        x_copy(source, 1).wait_recv()
        x_copy(source, -1).wait_recv()
        held = (
            sums[source, x].astype(f32)
            + x_in[0, source].astype(f32)
            + x_in[1, source].astype(f32)
        )
        far = (z < layers - 1) if way > 0 else (z > 0)

        @pl.when(far)
        def _():
            z_arrival(source).wait_recv()
            sums[source, x] = (held + z_in[source].astype(f32)).astype(bf16)

        @pl.when(jnp.logical_not(far))
        def _():
            sums[source, x] = held.astype(bf16)

        z_next(source, way).start()

    for step in range(layers - 1, -2, -1):
        both(step, merge_twin)
        if step == 0:
            for hop in (2, 1, 3):
                column = at.column(hop)
                twin_tile(hop).wait_recv()
                sums[z, column] = (
                    back[z, column, core].astype(f32) + e_in[column].astype(f32)
                ).astype(bf16)
                row_copy(hop).start()
        both(step + 1, merge_half)
        both(step + 2, merge_across)

    total[...] = selfs[...]
    twin_tile(0).wait_recv()
    total[core] += e_in[x].astype(f32)
    for hop in (1, 3, 2):
        row_copy(hop).wait_recv()
        tree = (at.column(-hop) < x).astype(jnp.int32)
        total[tree] += r_in[hop].astype(f32)

    @pl.when(z < layers - 1)
    def _():
        z_arrival(z).wait_recv()
        total[0] += z_in[z].astype(f32)

    @pl.when(z > 0)
    def _():
        z_arrival(layers).wait_recv()
        total[1] += z_in[layers].astype(f32)

    final[...] = total[...].astype(bf16)

    def regroup(step):
        peer = (at.y + step) % heads
        column = pl.ds(pl.multiple_of(at.y * HEAD_DIM, HEAD_DIM), HEAD_DIM)
        rows_k = pl.ds(pl.multiple_of(peer * share, share), share)
        rows_v = pl.ds(pl.multiple_of(BLOCK_TOKENS + peer * share, share), share)
        return (
            remote(final.at[:, rows_k, :], key_out.at[:, :, column],
                   y_send.at[2 * step], y_recv.at[2 * step], at.head_peer(step)),
            remote(final.at[:, rows_v, :], value_out.at[:, :, column],
                   y_send.at[2 * step + 1], y_recv.at[2 * step + 1], at.head_peer(step)),
        )

    for step in range(1, heads):
        for copy in regroup(step):
            copy.start()
    mine = pl.ds(pl.multiple_of(at.y * HEAD_DIM, HEAD_DIM), HEAD_DIM)
    key_out[:, :, mine] = final[:, pl.ds(pl.multiple_of(at.y * share, share), share), :]
    value_out[:, :, mine] = final[
        :, pl.ds(pl.multiple_of(BLOCK_TOKENS + at.y * share, share), share), :
    ]
    for step in range(1, heads):
        for copy in regroup(step):
            copy.wait()

    for step in range(X_CHIPS):
        twin_tile(step).wait_send()
    for hop in (1, 3, 2):
        row_copy(hop).wait_send()

    def drain(source, way):
        twin_row(source).wait_send()
        for step in (1, -1):
            x_half(source, step).wait_send()
            x_copy(source, step).wait_send()
        z_next(source, way).wait_send()

    for step in range(1, layers):
        both(step, drain)


def scatter_tiles(selfs, back, heads, leaves):
    layers = leaves // ROW
    dma = pltpu.SemaphoreType.DMA
    vmem = pl.BlockSpec(memory_space=pltpu.VMEM)
    bf16 = jnp.bfloat16
    share = BLOCK_TOKENS // heads
    out = jax.ShapeDtypeStruct((2, share, heads * HEAD_DIM), bf16)
    return pl.pallas_call(
        functools.partial(scatter_kernel, heads, leaves),
        out_shape=(out, out),
        in_specs=[vmem] * 2,
        out_specs=(vmem, vmem),
        scratch_shapes=[
            pltpu.VMEM((layers, X_CHIPS, KV_ROWS, HEAD_DIM), bf16),
            pltpu.VMEM((layers, X_CHIPS, KV_ROWS, HEAD_DIM), bf16),
            pltpu.VMEM((X_CHIPS, KV_ROWS, HEAD_DIM), bf16),
            pltpu.VMEM((2, layers, KV_ROWS, HEAD_DIM), bf16),
            pltpu.VMEM((2, layers, BLOCK_TOKENS, HEAD_DIM), bf16),
            pltpu.VMEM((X_CHIPS, KV_ROWS, HEAD_DIM), bf16),
            pltpu.VMEM((layers + 1, KV_ROWS, HEAD_DIM), bf16),
            pltpu.VMEM((2, KV_ROWS, HEAD_DIM), jnp.float32),
            pltpu.VMEM((2, KV_ROWS, HEAD_DIM), bf16),
            dma((2 * heads,)), dma((2 * heads,)),
            dma((layers,)), dma((layers + 1,)),
            dma((X_CHIPS,)), dma((X_CHIPS,)),
            dma((2, layers)), dma((2, layers)),
            dma((2, layers)), dma((2, layers)),
            dma((layers,)), dma((layers,)),
            dma((X_CHIPS,)), dma((X_CHIPS,)),
        ],
        compiler_params=pltpu.CompilerParams(
            collective_id=1, has_side_effects=True, vmem_limit_bytes=VMEM_LIMIT
        ),
        name="scatter_tiles",
    )(selfs, back)


def body(queries, keys, values, output_gradient, parents):
    heads, leaves = lax.axis_size("head"), lax.axis_size("leaf")
    marks = jnp.broadcast_to(
        parents.astype(jnp.bfloat16)[:, None, None], (2, PARENT_ROWS, HEAD_DIM)
    )
    own, buf = gather_tiles(keys, values, marks, heads, leaves)
    buf = buf.reshape(leaves, TILE_ROWS, HEAD_DIM)
    table = buf[:, KV_ROWS, 0].astype(jnp.int32)
    query_grads, selfs, back = attend(table, parents, queries, output_gradient, own, buf)
    back = back.reshape(leaves // ROW, X_CHIPS, 2, KV_ROWS, HEAD_DIM)
    key_gradient, value_gradient = scatter_tiles(selfs, back, heads, leaves)
    return query_grads, key_gradient, value_gradient


def solution(mesh):
    in_specs = (
        P("leaf", None, "head"),
        P("leaf", "head", None),
        P("leaf", "head", None),
        P("leaf", None, "head"),
        P("leaf"),
    )
    out_specs = (P("leaf", None, "head"), P("leaf", "head", None), P("leaf", "head", None))
    return jax.shard_map(body, mesh=mesh, in_specs=in_specs, out_specs=out_specs, check_vma=False)
```

time: 773 us -> 141 us (0.18); the launches traced: 757 us -> 140 us
  waiting for transfers between devices: 200 us -> 0 us
  matrix products: 172 us -> 0 us
  starting transfers between devices: 146 us -> 0 us
  Pallas kernels: 0 us -> 133 us
  loops' own time: 133 us -> 0 us
  local copies, waits for them, and re-layouts: 66.6 us -> 3.62 us
  other arithmetic: 38.5 us -> 3.31 us
    all_to_all x5 -> x0, waiting for transfers between devices: 200 us -> none  [the longest x3 103 us: in_one_piece(): lax.all_to_all(both, axis, split_axis=split_dim, concat_axis=concat_dim,...]
    dot_general x150 -> x0, matrix products: 172 us -> none  [the longest x42 42.2 us: slopes_of(): jnp.einsum('igrd,jgd->grij', grad_heads, block_values.reshape(-1, groups,...]
    all_to_all x5 -> x0, starting transfers between devices: 146 us -> none  [the longest x3 125 us: in_one_piece(): lax.all_to_all(both, axis, split_axis=split_dim, concat_axis=concat_dim,...]
    another operation x61 -> x0, loops' own time: 133 us -> none  [the longest x28 51.2 us: second(): lax.cond(anc_block >= 0, second_active, lambda status: status, carry_in)]
    pallas_call x0 -> x3, Pallas kernels: none -> 133 us  [the longest x1 54.9 us: gather_tiles(): pl.pallas_call(functools.partial(gather_kernel, heads, leaves), out_shape...]
    dynamic_slice x57 -> x0, local copies, waits for them, and re-layouts: 32.6 us -> none  [the longest x28 16.4 us: first_sweep(): anc_block = chain_row[link_no]]
    another operation x31 -> x0, other arithmetic: 22.2 us -> none
    gather x14 -> x0, local copies, waits for them, and re-layouts: 17.2 us -> none  [extend(): upward = jnp.where(current >= 0, parent_table[jnp.maximum(current, 0)], -1)]
  transfers between devices with their start and end apart: 5 -> 0, of which waited for: 4 -> 0; matrix products, arithmetic and copies ran while one was open for 6% -> 0% of each run, Pallas kernels for 0% -> 0%
where the time goes in v1:
time: 141 us; the launch traced here: 140 us
  Pallas kernels  133 us (94%)
  local copies, waits for them, and re-layouts  3.62 us (3%)
  other arithmetic  3.31 us (2%)
    pallas_call x1, Pallas kernels, gather_tiles(): pl.pallas_call(functools.partial(gather_kernel, heads, leaves), out_shape...  54.9 us
    pallas_call x1, Pallas kernels, scatter_tiles(): pl.pallas_call(functools.partial(scatter_kernel, heads, leaves), out_shap...  48.4 us
    pallas_call x1, Pallas kernels, attend(): pl.pallas_call(attend_kernel, out_shape=(jax.ShapeDtypeStruct(queries.sha...  29.4 us
    unnamed x2, local copies, waits for them, and re-layouts  2.95 us

profile of v1, /device:TPU:6, one launch (start us, length us, event | category | flops | bytes accessed | tf_op | source)
XLA Modules:
  0.0 140.3 jit_solution(679025833494985006)
XLA Ops:
  0.6 0.7 convert_element_type.8
  1.3 0.7 broadcast_in_dim.2.marks
  2.0 54.9 %gather_tiles.1 = (bf16[2,272,128]{2,1,0:T(8,128)(2,1)}, bf16[8,4,2,272,128]{4,3,2,1,0:T(8,128)(2,1)}) custom-call(bf16[2,16,1024]{2,1,0:T(8,128)(2,1)} %keys.1, bf16[2,16,1024]{2,1,0:T(8,128)(2,1)} %values.1, bf16[2,16,128]{2,1,0:T(8,128)(2,1)} %broadcast_in_dim.2.marks), custom_call_target="tpu_custom_call" | custom-call | tf_op jit(solution)/shard_map/gather_tiles/pallas_call | solution.py:241
  56.9 2.6 %fusion.table = s32[64]{0:T(128)} fusion(bf16[64,272,128]{2,1,0:T(8,128)(2,1)} %bitcast.3), kind=kLoop, calls=%fused_computation.1 | loop fusion | flops 64 | bytes 384 | tf_op jit(solution)/shard_map/convert_element_type | solution.py:646
  59.5 29.4 %attend.1 = (bf16[2,128,1024]{2,1,0:T(8,128)(2,1)}, f32[2,256,128]{2,1,0:T(8,128)}, bf16[64,256,128]{2,1,0:T(8,128)(2,1)}) custom-call(s32[64]{0:T(128)} %fusion.table, s32[2]{0:T(128)} %first.1, bf16[2,128,1024]{2,1,0:T(8,128)(2,1)} %queries.1, bf16[2,128,1024]{2,1,0:T(8,128)(2,1)} %grads.1, bf16[2,272,128]{2,1,0:T(8,128)(2,1)} %get-tuple-element.11.own, ...), custom_call_target="tpu_custom_call" | custom-call | flops 5033164800 | bytes 12582912 | tf_op jit(solution)/shard_map/attend/pallas_call | solution.py:398
  88.9 48.4 %scatter_tiles.1 = (bf16[2,16,1024]{2,1,0:T(8,128)(2,1)}, bf16[2,16,1024]{2,1,0:T(8,128)(2,1)}) custom-call(f32[2,256,128]{2,1,0:T(8,128)} %get-tuple-element.13.selfs, bf16[8,4,2,256,128]{4,3,2,1,0:T(8,128)(2,1)} %bitcast.2), custom_call_target="tpu_custom_call" | custom-call | tf_op jit(solution)/shard_map/scatter_tiles/pallas_call | solution.py:609
  137.3 1.5 %copy.10 = bf16[2,16,1024]{2,1,0:T(8,128)(2,1)} copy(bf16[2,16,1024]{2,1,0:T(8,128)(2,1)} %get-tuple-element.21) | data formatting | bytes 131072
  138.8 1.5 %copy.11 = bf16[2,16,1024]{2,1,0:T(8,128)(2,1)} copy(bf16[2,16,1024]{2,1,0:T(8,128)(2,1)} %get-tuple-element.22) | data formatting | bytes 131072

commit v2 on v1

--- a/solution.py
+++ b/solution.py
@@ -44,7 +44,8 @@
         return (self.y, self.leaf_of(self.z, self.column(step), self.core))
 
     def along_z(self, step):
-        return (self.y, self.leaf_of(self.z + step, self.x, self.core))
+        layer = (self.z + step + self.layers) % self.layers
+        return (self.y, self.leaf_of(layer, self.x, self.core))
 
     def sibling(self):
         return (self.y, self.leaf_of(self.z, self.x, 1 - self.core))
@@ -64,16 +65,9 @@
             signal(self.along_x(step))
         signal(self.sibling())
 
-        @pl.when(self.z > 0)
-        def _():
-            signal(self.along_z(-1))
-
-        @pl.when(self.z < self.layers - 1)
-        def _():
-            signal(self.along_z(1))
-
-        inner = ((self.z > 0) & (self.z < self.layers - 1)).astype(jnp.int32)
-        pl.semaphore_wait(barrier, self.heads - 1 + X_CHIPS - 1 + 1 + 1 + inner)
+        for step in range(1, self.layers):
+            signal(self.along_z(step))
+        pl.semaphore_wait(barrier, self.heads + self.layers + X_CHIPS - 2)
 
 
 def remote(src, dst, send_sem, recv_sem, device):
@@ -84,7 +78,7 @@
 
 
 def gather_kernel(
-    heads, leaves, keys, values, marks, own, buf,
+    heads, leaves, parents, keys, values, own, buf,
     y_send, y_recv, z_send, z_recv, r_send, r_recv, x_send, x_recv, h_send, h_recv,
     d_send, d_recv, e_send, e_recv,
 ):
@@ -111,7 +105,10 @@
     mine = pl.ds(pl.multiple_of(at.y * HEAD_DIM, HEAD_DIM), HEAD_DIM)
     own[:, pl.ds(pl.multiple_of(at.y * share, share), share), :] = keys[:, :, mine]
     own[:, pl.ds(pl.multiple_of(BLOCK_TOKENS + at.y * share, share), share), :] = values[:, :, mine]
-    own[:, KV_ROWS:, :] = marks[...]
+    for tree in range(2):
+        own[tree, KV_ROWS:, :] = jnp.full(
+            (PARENT_ROWS, HEAD_DIM), parents[tree].astype(jnp.float32), jnp.float32
+        ).astype(jnp.bfloat16)
     for step in range(1, heads):
         for copy in regroup(step):
             copy.wait_recv()
@@ -119,17 +116,17 @@
     def slot(zz, xx, cc):
         return buf.at[zz, xx, cc]
 
-    up_send = z_send.at[layers]
-    down_send = z_send.at[layers + 1]
-
-    def first_up():
-        return remote(own.at[0], slot(z, x, core), up_send, z_recv.at[z], at.along_z(1))
-
-    def first_down():
-        return remote(own.at[1], slot(z, x, core), down_send, z_recv.at[z], at.along_z(-1))
-
-    pl.when(z < layers - 1)(lambda: first_up().start())
-    pl.when(z > 0)(lambda: first_down().start())
+    def layer_copy(step):
+        target = (z + step + layers) % layers
+        tree = (target < z).astype(jnp.int32)
+        return remote(own.at[tree], slot(z, x, core), z_send.at[step % layers], z_recv.at[z],
+                      at.along_z(step))
+
+    nearest_first = []
+    for step in range(1, layers // 2 + 1):
+        nearest_first += [step] if 2 * step == layers else [step, -step]
+    for step in nearest_first:
+        layer_copy(step).start()
 
     def row_copy(step):
         tree = (at.column(step) < x).astype(jnp.int32)
@@ -150,11 +147,7 @@
 
     def z_arrival(source):
         tile = slot(source, x, core)
-        return remote(tile, tile, z_send.at[source], z_recv.at[source], at.sibling())
-
-    def z_next(source, step):
-        tile = slot(source, x, core)
-        return remote(tile, tile, z_send.at[source], z_recv.at[source], at.along_z(step))
+        return remote(tile, tile, z_send.at[0], z_recv.at[source], at.sibling())
 
     def x_copy(source, step):
         tile = slot(source, x, core)
@@ -181,8 +174,6 @@
 
     def arrive(source, way):
         z_arrival(source).wait_recv()
-        more = (z < layers - 1) if way > 0 else (z > 0)
-        pl.when(more)(lambda: z_next(source, way).start())
         x_copy(source, 1).start()
         x_copy(source, -1).start()
 
@@ -215,16 +206,14 @@
     for step in range(1, heads):
         for copy in regroup(step):
             copy.wait_send()
-    pl.when(z < layers - 1)(lambda: first_up().wait_send())
-    pl.when(z > 0)(lambda: first_down().wait_send())
+    for step in nearest_first:
+        layer_copy(step).wait_send()
     twin_copy().wait_send()
     for hop in (1, 3, 2):
         row_copy(hop).wait_send()
         row_from(hop).wait_send()
 
     def drain(source, way):
-        more = (z < layers - 1) if way > 0 else (z > 0)
-        pl.when(more)(lambda: z_next(source, way).wait_send())
         for step in (1, -1):
             x_copy(source, step).wait_send()
             x_half(source, step).wait_send()
@@ -234,7 +223,7 @@
         both(step, drain)
 
 
-def gather_tiles(keys, values, marks, heads, leaves):
+def gather_tiles(parents, keys, values, heads, leaves):
     layers = leaves // ROW
     dma = pltpu.SemaphoreType.DMA
     vmem = pl.BlockSpec(memory_space=pltpu.VMEM)
@@ -244,11 +233,11 @@
             jax.ShapeDtypeStruct((2, TILE_ROWS, HEAD_DIM), jnp.bfloat16),
             jax.ShapeDtypeStruct((layers, X_CHIPS, 2, TILE_ROWS, HEAD_DIM), jnp.bfloat16),
         ),
-        in_specs=[vmem] * 3,
+        in_specs=[pl.BlockSpec(memory_space=pltpu.SMEM), vmem, vmem],
         out_specs=(vmem, vmem),
         scratch_shapes=[
             dma((2 * heads,)), dma((2 * heads,)),
-            dma((layers + 2,)), dma((layers,)),
+            dma((layers,)), dma((layers,)),
             dma((X_CHIPS,)), dma((X_CHIPS,)),
             dma((2, layers)), dma((2, layers)),
             dma((2, layers)), dma((2, layers)),
@@ -259,7 +248,7 @@
             collective_id=0, has_side_effects=True, vmem_limit_bytes=VMEM_LIMIT
         ),
         name="gather_tiles",
-    )(keys, values, marks)
+    )(parents, keys, values)
 
 
 LANES = 2 * BLOCK_TOKENS
@@ -269,14 +258,21 @@
 
 
 def attend_kernel(
-    table, first, queries, grads, own, buf, dq, selfs, back,
-    kcat, vcat, kcat_t, q2, g2, s_scr, l_scr, p_all, d_all,
+    first, queries, grads, own, buf, dq, selfs, back,
+    kcat, vcat, kcat_t, q2, g2, s_scr, l_scr, p_all, d_all, links, table, table_sem,
 ):
     softmax_scale = HEAD_DIM ** -0.5
     log2_scale = softmax_scale * 1.4426950408889634
     rows = HEADS_PER_GROUP * BLOCK_TOKENS
     nt = (((1,), (1,)), ((), ()))
+    leaves = buf.shape[0]
+    marks = buf[:, KV_ROWS:KV_ROWS + 8, :][:, 0, :].astype(jnp.float32)
+    marks = jnp.concatenate([marks, jnp.zeros((HEAD_DIM - leaves, HEAD_DIM), jnp.float32)]).T
+    links[...] = marks[:8].astype(jnp.int32)
+    to_scalars = pltpu.make_async_copy(links, table, table_sem)
+    to_scalars.start()
     back[...] = jnp.zeros_like(back)
+    to_scalars.wait()
 
     def one_tree(tree, carry):
         kcat[:BLOCK_TOKENS] = own[tree, :BLOCK_TOKENS]
@@ -300,7 +296,7 @@
 
             alive.append(active)
             ranks.append(rank)
-            current = jnp.where(active, table[rank], -1)
+            current = jnp.where(active, table[0, rank], -1)
         for link in range(CHAIN):
             place = slice(link * BLOCK_TOKENS, (link + 1) * BLOCK_TOKENS)
             kcat_t[:, place] = kcat[place].T
@@ -313,57 +309,76 @@
         row_pos = lax.broadcasted_iota(jnp.int32, (BLOCK_TOKENS, LANES), 1) % BLOCK_TOKENS
         causal = key_pos <= row_pos
 
-        def head_pair(pair, carry):
-            lanes = pl.ds(pl.multiple_of(pair * LANES, LANES), LANES)
-            q_pair = q2[lanes]
-            g_pair = g2[lanes]
-            peak = None
-            for part in range(PARTS):
-                place = slice(part * PART, (part + 1) * PART)
-                raw = lax.dot_general(kcat[place], q_pair, nt, preferred_element_type=jnp.float32)
-                l_scr[place] = lax.dot_general(
-                    vcat[place], g_pair, nt, preferred_element_type=jnp.float32
-                )
-                for block in range(PART // BLOCK_TOKENS):
-                    link = part * (PART // BLOCK_TOKENS) + block
-                    score = raw[block * BLOCK_TOKENS:(block + 1) * BLOCK_TOKENS] * log2_scale
-                    if link == 0:
-                        score = jnp.where(causal, score, masked_score)
-                    else:
-                        score = score + jnp.where(alive[link - 1], 0.0, masked_score)
-                    s_scr[link * BLOCK_TOKENS:(link + 1) * BLOCK_TOKENS] = score
-                    top = jnp.max(score.reshape(BLOCK_TOKENS // 8, 8, LANES), 0)
-                    peak = top if peak is None else jnp.maximum(peak, top)
+        bias = [jnp.float32(0.0)] + [jnp.where(on, 0.0, masked_score) for on in alive]
+
+        def lanes_of(pair):
+            return slice(pair * LANES, (pair + 1) * LANES)
+
+        def place_of(link):
+            return slice(link * BLOCK_TOKENS, (link + 1) * BLOCK_TOKENS)
+
+        def score_block(pair, link, peak):
+            place, lanes, turn = place_of(link), lanes_of(pair), pair % 2
+            raw = lax.dot_general(kcat[place], q2[lanes], nt, preferred_element_type=jnp.float32)
+            if link == 0:
+                raw = jnp.where(causal, raw, masked_score)
+            s_scr[turn, place] = raw
+            l_scr[turn, place] = lax.dot_general(
+                vcat[place], g2[lanes], nt, preferred_element_type=jnp.float32
+            )
+            top = jnp.max(raw.reshape(-1, 8, LANES), 0) * log2_scale + bias[link]
+            return top if peak is None else jnp.maximum(peak, top)
+
+        def sum_block(pair, link, peak, total, lean):
+            turn = pair % 2
+            offset = jnp.broadcast_to(bias[link] - peak, (16, LANES))
+            for row in range(link * BLOCK_TOKENS, (link + 1) * BLOCK_TOKENS, 16):
+                slab = slice(row, row + 16)
+                shifted = jnp.exp2(s_scr[turn, slab] * log2_scale + offset)
+                s_scr[turn, slab] = shifted
+                total = total + shifted
+                lean = lean + shifted * l_scr[turn, slab]
+            return total, lean
+
+        def weight_block(pair, link, inverse, mean):
+            lanes, turn = lanes_of(pair), pair % 2
+            for row in range(link * BLOCK_TOKENS, (link + 1) * BLOCK_TOKENS, 16):
+                slab = slice(row, row + 16)
+                weights = s_scr[turn, slab] * inverse
+                d_all[slab, lanes] = (weights * (l_scr[turn, slab] - mean)).astype(jnp.bfloat16)
+                p_all[slab, lanes] = weights.astype(jnp.bfloat16)
+
+        def query_part(pair):
+            part = jnp.dot(
+                kcat_t[...], d_all[:, lanes_of(pair)], preferred_element_type=jnp.float32
+            )
+            part = (part * softmax_scale).T.astype(jnp.bfloat16)
+            for half in range(2):
+                head = 2 * pair + half
+                dq[tree, :, place_of(head)] = part[place_of(half)]
+
+        pairs = rows // LANES
+        peak = None
+        for link in range(CHAIN):
+            peak = score_block(0, link, peak)
+        for pair in range(pairs):
             peak = jnp.max(peak, 0, keepdims=True)
-            total = jnp.zeros((8, LANES), jnp.float32)
-            lean = jnp.zeros((8, LANES), jnp.float32)
+            total = jnp.zeros((16, LANES), jnp.float32)
+            lean = jnp.zeros((16, LANES), jnp.float32)
+            later = None
+            half = (CHAIN + 1) // 2
             for link in range(CHAIN):
-                place = slice(link * BLOCK_TOKENS, (link + 1) * BLOCK_TOKENS)
-                shifted = jnp.exp2(s_scr[place] - peak)
-                s_scr[place] = shifted
-                total = total + jnp.sum(shifted.reshape(-1, 8, LANES), 0)
-                lean = lean + jnp.sum((shifted * l_scr[place]).reshape(-1, 8, LANES), 0)
+                total, lean = sum_block(pair, link, peak, total, lean)
+                if pair + 1 < pairs and link % 2 == 0:
+                    later = score_block(pair + 1, link // 2, later)
             inverse = 1.0 / jnp.sum(total, 0, keepdims=True)
             mean = jnp.sum(lean, 0, keepdims=True) * inverse
-            query_part = jnp.zeros((HEAD_DIM, LANES), jnp.float32)
-            for part in range(PARTS):
-                place = slice(part * PART, (part + 1) * PART)
-                weights = s_scr[place] * inverse
-                dscore = (weights * (l_scr[place] - mean)).astype(jnp.bfloat16)
-                p_all[place, lanes] = weights.astype(jnp.bfloat16)
-                d_all[place, lanes] = dscore
-                query_part = query_part + jnp.dot(
-                    kcat_t[:, place], dscore, preferred_element_type=jnp.float32
-                )
-            query_part = (query_part * softmax_scale).T.astype(jnp.bfloat16)
-            for half in range(2):
-                column = pl.multiple_of(pair * LANES + half * HEAD_DIM, HEAD_DIM)
-                dq[tree, :, pl.ds(column, HEAD_DIM)] = query_part[
-                    half * BLOCK_TOKENS:(half + 1) * BLOCK_TOKENS
-                ]
-            return carry
-
-        lax.fori_loop(0, rows // LANES, head_pair, 0)
+            for link in range(CHAIN):
+                weight_block(pair, link, inverse, mean)
+                if pair + 1 < pairs and link % 2 == 1:
+                    later = score_block(pair + 1, half + link // 2, later)
+            query_part(pair)
+            peak = later
 
         for part in range(PARTS):
             place = slice(part * PART, (part + 1) * PART)
@@ -389,7 +404,7 @@
     lax.fori_loop(0, 2, one_tree, 0)
 
 
-def attend(table, first, queries, grads, own, buf):
+def attend(first, queries, grads, own, buf):
     leaves = buf.shape[0]
     rows = HEADS_PER_GROUP * BLOCK_TOKENS
     vmem = pl.BlockSpec(memory_space=pltpu.VMEM)
@@ -402,7 +417,7 @@
             jax.ShapeDtypeStruct((2, KV_ROWS, HEAD_DIM), f32),
             jax.ShapeDtypeStruct((leaves, KV_ROWS, HEAD_DIM), bf16),
         ),
-        in_specs=[smem, smem, vmem, vmem, vmem, vmem],
+        in_specs=[smem, vmem, vmem, vmem, vmem],
         out_specs=(vmem, vmem, vmem),
         scratch_shapes=[
             pltpu.VMEM((SPAN, HEAD_DIM), bf16),
@@ -410,10 +425,13 @@
             pltpu.VMEM((HEAD_DIM, SPAN), bf16),
             pltpu.VMEM((rows, HEAD_DIM), bf16),
             pltpu.VMEM((rows, HEAD_DIM), bf16),
-            pltpu.VMEM((SPAN, LANES), f32),
-            pltpu.VMEM((SPAN, LANES), f32),
+            pltpu.VMEM((2, SPAN, LANES), f32),
+            pltpu.VMEM((2, SPAN, LANES), f32),
             pltpu.VMEM((SPAN, rows), bf16),
             pltpu.VMEM((SPAN, rows), bf16),
+            pltpu.VMEM((8, HEAD_DIM), jnp.int32),
+            pltpu.SMEM((8, HEAD_DIM), jnp.int32),
+            pltpu.SemaphoreType.DMA,
         ],
         compiler_params=pltpu.CompilerParams(vmem_limit_bytes=VMEM_LIMIT),
         cost_estimate=pl.CostEstimate(
@@ -421,7 +439,7 @@
             transcendentals=2 * SPAN * rows,
         ),
         name="attend",
-    )(table, first, queries, grads, own, buf)
+    )(first, queries, grads, own, buf)
 
 
 def scatter_kernel(
@@ -470,13 +488,13 @@
         return remote(sums.at[source, at.column(step)], x_in.at[side, source],
                       x_send.at[side, source], x_recv.at[side, source], at.along_x(step))
 
-    def z_next(source, way):
-        place = source if way > 0 else jnp.where(source == z + 1, layers, source)
-        return remote(sums.at[source, x], z_in.at[place], z_send.at[source], z_recv.at[place],
-                      at.along_z(-way))
-
-    def z_arrival(place):
-        return remote(z_in.at[place], z_in.at[place], z_send.at[z], z_recv.at[place], at.sibling())
+    def z_home(source, way):
+        return remote(sums.at[source, x], z_in.at[z], z_send.at[source], z_recv.at[z],
+                      (at.y, at.leaf_of(source, x, core)))
+
+    def z_arrival(source):
+        return remote(z_in.at[source], z_in.at[source], z_send.at[z], z_recv.at[source],
+                      at.sibling())
 
     def row_copy(step):
         return remote(sums.at[z, at.column(step)], r_in.at[step], r_send.at[step],
@@ -508,23 +526,12 @@
     def merge_across(source, way):
         x_copy(source, 1).wait_recv()
         x_copy(source, -1).wait_recv()
-        held = (
+        sums[source, x] = (
             sums[source, x].astype(f32)
             + x_in[0, source].astype(f32)
             + x_in[1, source].astype(f32)
-        )
-        far = (z < layers - 1) if way > 0 else (z > 0)
-
-        @pl.when(far)
-        def _():
-            z_arrival(source).wait_recv()
-            sums[source, x] = (held + z_in[source].astype(f32)).astype(bf16)
-
-        @pl.when(jnp.logical_not(far))
-        def _():
-            sums[source, x] = held.astype(bf16)
-
-        z_next(source, way).start()
+        ).astype(bf16)
+        z_home(source, way).start()
 
     for step in range(layers - 1, -2, -1):
         both(step, merge_twin)
@@ -547,15 +554,13 @@
         tree = (at.column(-hop) < x).astype(jnp.int32)
         total[tree] += r_in[hop].astype(f32)
 
-    @pl.when(z < layers - 1)
-    def _():
-        z_arrival(z).wait_recv()
-        total[0] += z_in[z].astype(f32)
-
-    @pl.when(z > 0)
-    def _():
-        z_arrival(layers).wait_recv()
-        total[1] += z_in[layers].astype(f32)
+    def take(source, way):
+        z_arrival(source).wait_recv()
+        tree = (source < z).astype(jnp.int32)
+        total[tree] += z_in[source].astype(f32)
+
+    for step in range(layers - 1, 0, -1):
+        both(step, take)
 
     final[...] = total[...].astype(bf16)
 
@@ -593,7 +598,7 @@
         for step in (1, -1):
             x_half(source, step).wait_send()
             x_copy(source, step).wait_send()
-        z_next(source, way).wait_send()
+        z_home(source, way).wait_send()
 
     for step in range(1, layers):
         both(step, drain)
@@ -618,11 +623,11 @@
             pltpu.VMEM((2, layers, KV_ROWS, HEAD_DIM), bf16),
             pltpu.VMEM((2, layers, BLOCK_TOKENS, HEAD_DIM), bf16),
             pltpu.VMEM((X_CHIPS, KV_ROWS, HEAD_DIM), bf16),
-            pltpu.VMEM((layers + 1, KV_ROWS, HEAD_DIM), bf16),
+            pltpu.VMEM((layers, KV_ROWS, HEAD_DIM), bf16),
             pltpu.VMEM((2, KV_ROWS, HEAD_DIM), jnp.float32),
             pltpu.VMEM((2, KV_ROWS, HEAD_DIM), bf16),
             dma((2 * heads,)), dma((2 * heads,)),
-            dma((layers,)), dma((layers + 1,)),
+            dma((layers,)), dma((layers,)),
             dma((X_CHIPS,)), dma((X_CHIPS,)),
             dma((2, layers)), dma((2, layers)),
             dma((2, layers)), dma((2, layers)),
@@ -638,13 +643,9 @@
 
 def body(queries, keys, values, output_gradient, parents):
     heads, leaves = lax.axis_size("head"), lax.axis_size("leaf")
-    marks = jnp.broadcast_to(
-        parents.astype(jnp.bfloat16)[:, None, None], (2, PARENT_ROWS, HEAD_DIM)
-    )
-    own, buf = gather_tiles(keys, values, marks, heads, leaves)
+    own, buf = gather_tiles(parents, keys, values, heads, leaves)
     buf = buf.reshape(leaves, TILE_ROWS, HEAD_DIM)
-    table = buf[:, KV_ROWS, 0].astype(jnp.int32)
-    query_grads, selfs, back = attend(table, parents, queries, output_gradient, own, buf)
+    query_grads, selfs, back = attend(parents, queries, output_gradient, own, buf)
     back = back.reshape(leaves // ROW, X_CHIPS, 2, KV_ROWS, HEAD_DIM)
     key_gradient, value_gradient = scatter_tiles(selfs, back, heads, leaves)
     return query_grads, key_gradient, value_gradient

time: 141 us -> 123 us (0.87)
  the two profiles are of different devices: /device:TPU:6 before, /device:TPU:80 now
where the time goes in v2:
time: 123 us
  Pallas kernels  119 us (97%)
  local copies, waits for them, and re-layouts  2.95 us (2%)
    pallas_call x1, Pallas kernels, gather_tiles(): pl.pallas_call(functools.partial(gather_kernel, heads, leaves), out_shape...  48.9 us
    pallas_call x1, Pallas kernels, scatter_tiles(): pl.pallas_call(functools.partial(scatter_kernel, heads, leaves), out_shap...  47.2 us
    pallas_call x1, Pallas kernels, attend(): pl.pallas_call(attend_kernel, out_shape=(jax.ShapeDtypeStruct(queries.sha...  23.3 us
    unnamed x2, local copies, waits for them, and re-layouts  2.95 us

profile of v2, /device:TPU:80, one launch (start us, length us, event | category | flops | bytes accessed | tf_op | source)
XLA Modules:
  0.0 123.0 jit_solution(7955457132711853499)
XLA Ops:
  0.6 48.9 %gather_tiles.1 = (bf16[2,272,128]{2,1,0:T(8,128)(2,1)}, bf16[8,4,2,272,128]{4,3,2,1,0:T(8,128)(2,1)}) custom-call(s32[2]{0:T(128)} %first.1, bf16[2,16,1024]{2,1,0:T(8,128)(2,1)} %keys.1, bf16[2,16,1024]{2,1,0:T(8,128)(2,1)} %values.1), custom_call_target="tpu_custom_call" | custom-call | tf_op jit(solution)/shard_map/gather_tiles/pallas_call | solution.py:230
  49.6 23.3 %attend.1 = (bf16[2,128,1024]{2,1,0:T(8,128)(2,1)}, f32[2,256,128]{2,1,0:T(8,128)}, bf16[64,256,128]{2,1,0:T(8,128)(2,1)}) custom-call(s32[2]{0:T(128)} %first.1, bf16[2,128,1024]{2,1,0:T(8,128)(2,1)} %queries.1, bf16[2,128,1024]{2,1,0:T(8,128)(2,1)} %grads.1, bf16[2,272,128]{2,1,0:T(8,128)(2,1)} %get-tuple-element.10.own, bf16[64,272,128]{2,1,0:T(8,128)(2,1)} %bitcast.3), custom_call_target="tpu_custom_call" | custom-call | flops 5033164800 | bytes 12582912 | tf_op jit(solution)/shard_map/attend/pallas_call | solution.py:413
  72.9 47.2 %scatter_tiles.1 = (bf16[2,16,1024]{2,1,0:T(8,128)(2,1)}, bf16[2,16,1024]{2,1,0:T(8,128)(2,1)}) custom-call(f32[2,256,128]{2,1,0:T(8,128)} %get-tuple-element.13.selfs, bf16[8,4,2,256,128]{4,3,2,1,0:T(8,128)(2,1)} %bitcast.2), custom_call_target="tpu_custom_call" | custom-call | tf_op jit(solution)/shard_map/scatter_tiles/pallas_call | solution.py:614
  120.1 1.5 %copy.10 = bf16[2,16,1024]{2,1,0:T(8,128)(2,1)} copy(bf16[2,16,1024]{2,1,0:T(8,128)(2,1)} %get-tuple-element.21) | data formatting | bytes 131072
  121.6 1.5 %copy.11 = bf16[2,16,1024]{2,1,0:T(8,128)(2,1)} copy(bf16[2,16,1024]{2,1,0:T(8,128)(2,1)} %get-tuple-element.22) | data formatting | bytes 131072

commit v3 on v2

--- a/solution.py
+++ b/solution.py
@@ -20,7 +20,9 @@
 PARENT_ROWS = 16
 KV_ROWS = 2 * BLOCK_TOKENS
 TILE_ROWS = KV_ROWS + PARENT_ROWS
-VMEM_LIMIT = 56 * 1024 * 1024
+GATHER_VMEM = 10 * 1024 * 1024
+ATTEND_VMEM = 30 * 1024 * 1024
+SCATTER_VMEM = 18 * 1024 * 1024
 masked_score = -1e30
 MESH = pl.DeviceIdType.MESH
 
@@ -52,6 +54,13 @@
 
     def head_peer(self, step):
         return ((self.y + step) % self.heads, self.leaf)
+
+    def layers_at(self, distance):
+        if distance < 1 or 2 * distance > self.layers:
+            return []
+        below = (self.z - distance + self.layers) % self.layers
+        above = (self.z + distance) % self.layers
+        return [below] if 2 * distance == self.layers else [below, above]
 
     def greet(self):
         barrier = pltpu.get_barrier_semaphore()
@@ -166,42 +175,41 @@
         part = buf.at[source, :, core]
         return remote(part, part, d_send.at[source], d_recv.at[source], at.sibling())
 
-    def both(step, action):
-        if step < 1 or step > layers - 1:
-            return
-        pl.when(z - step >= 0)(lambda: action(z - step, 1))
-        pl.when(z + step <= layers - 1)(lambda: action(z + step, -1))
-
-    def arrive(source, way):
+    def each(distance, action):
+        for source in at.layers_at(distance):
+            action(source)
+
+    def arrive(source):
         z_arrival(source).wait_recv()
         x_copy(source, 1).start()
         x_copy(source, -1).start()
 
-    def across(source, way):
+    def across(source):
         x_copy(source, 1).wait_recv()
         x_half(source, 1).start()
         x_copy(source, -1).wait_recv()
         x_half(source, -1).start()
 
-    def share_row(source, way):
+    def share_row(source):
         x_half(source, 1).wait_recv()
         x_half(source, -1).wait_recv()
         twin_row(source).start()
 
-    for step in range(1, layers + 2):
-        both(step, arrive)
+    reach = layers // 2
+    for step in range(1, reach + 3):
+        each(step, arrive)
         if step == 1:
             for hop in (1, 3, 2):
                 row_copy(hop).wait_recv()
                 row_from(hop).start()
-        both(step - 1, across)
-        both(step - 2, share_row)
+        each(step - 1, across)
+        each(step - 2, share_row)
 
     twin_copy().wait_recv()
     for hop in (1, 3, 2):
         row_from(hop).wait_recv()
-    for step in range(1, layers):
-        both(step, lambda source, way: twin_row(source).wait_recv())
+    for step in range(1, reach + 1):
+        each(step, lambda source: twin_row(source).wait_recv())
 
     for step in range(1, heads):
         for copy in regroup(step):
@@ -213,14 +221,14 @@
         row_copy(hop).wait_send()
         row_from(hop).wait_send()
 
-    def drain(source, way):
+    def drain(source):
         for step in (1, -1):
             x_copy(source, step).wait_send()
             x_half(source, step).wait_send()
         twin_row(source).wait_send()
 
-    for step in range(1, layers):
-        both(step, drain)
+    for step in range(1, layers // 2 + 1):
+        each(step, drain)
 
 
 def gather_tiles(parents, keys, values, heads, leaves):
@@ -245,7 +253,10 @@
             dma((X_CHIPS,)), dma((X_CHIPS,)),
         ],
         compiler_params=pltpu.CompilerParams(
-            collective_id=0, has_side_effects=True, vmem_limit_bytes=VMEM_LIMIT
+            collective_id=0, has_side_effects=True, vmem_limit_bytes=GATHER_VMEM
+        ),
+        cost_estimate=pl.CostEstimate(
+            flops=1 << 34, bytes_accessed=8 << 20, transcendentals=0
         ),
         name="gather_tiles",
     )(parents, keys, values)
@@ -433,7 +444,7 @@
             pltpu.SMEM((8, HEAD_DIM), jnp.int32),
             pltpu.SemaphoreType.DMA,
         ],
-        compiler_params=pltpu.CompilerParams(vmem_limit_bytes=VMEM_LIMIT),
+        compiler_params=pltpu.CompilerParams(vmem_limit_bytes=ATTEND_VMEM),
         cost_estimate=pl.CostEstimate(
             flops=10 * SPAN * rows * HEAD_DIM * 2, bytes_accessed=12 << 20,
             transcendentals=2 * SPAN * rows,
@@ -454,11 +465,9 @@
     f32, bf16 = jnp.float32, jnp.bfloat16
     at.greet()
 
-    def both(step, action):
-        if step < 1 or step > layers - 1:
-            return
-        pl.when(z - step >= 0)(lambda: action(z - step, 1))
-        pl.when(z + step <= layers - 1)(lambda: action(z + step, -1))
+    def each(distance, action):
+        for source in at.layers_at(distance):
+            action(source)
 
     def twin_row(source):
         return remote(back.at[source, :, 1 - core], d_in.at[source], d_send.at[source],
@@ -469,8 +478,9 @@
         return remote(back.at[z, column, 1 - core], e_in.at[column],
                       e_send.at[step], e_recv.at[step], at.sibling())
 
-    for step in range(layers - 1, 0, -1):
-        both(step, lambda source, way: twin_row(source).start())
+    reach = layers // 2
+    for step in range(reach, 0, -1):
+        each(step, lambda source: twin_row(source).start())
     for step in range(X_CHIPS):
         twin_tile(step).start()
 
@@ -488,7 +498,7 @@
         return remote(sums.at[source, at.column(step)], x_in.at[side, source],
                       x_send.at[side, source], x_recv.at[side, source], at.along_x(step))
 
-    def z_home(source, way):
+    def z_home(source):
         return remote(sums.at[source, x], z_in.at[z], z_send.at[source], z_recv.at[z],
                       (at.y, at.leaf_of(source, x, core)))
 
@@ -500,7 +510,7 @@
         return remote(sums.at[z, at.column(step)], r_in.at[step], r_send.at[step],
                       r_recv.at[step], at.along_x(step))
 
-    def merge_twin(source, way):
+    def merge_twin(source):
         twin_row(source).wait_recv()
         for column in range(X_CHIPS):
             sums[source, column] = (
@@ -509,7 +519,7 @@
         x_half(source, 1).start()
         x_half(source, -1).start()
 
-    def merge_half(source, way):
+    def merge_half(source):
         x_half(source, 1).wait_recv()
         right = at.column(1)
         sums[source, right, values_half] = (
@@ -523,7 +533,7 @@
         ).astype(bf16)
         x_copy(source, -1).start()
 
-    def merge_across(source, way):
+    def merge_across(source):
         x_copy(source, 1).wait_recv()
         x_copy(source, -1).wait_recv()
         sums[source, x] = (
@@ -531,10 +541,10 @@
             + x_in[0, source].astype(f32)
             + x_in[1, source].astype(f32)
         ).astype(bf16)
-        z_home(source, way).start()
-
-    for step in range(layers - 1, -2, -1):
-        both(step, merge_twin)
+        z_home(source).start()
+
+    for step in range(reach, -2, -1):
+        each(step, merge_twin)
         if step == 0:
             for hop in (2, 1, 3):
                 column = at.column(hop)
@@ -543,8 +553,8 @@
                     back[z, column, core].astype(f32) + e_in[column].astype(f32)
                 ).astype(bf16)
                 row_copy(hop).start()
-        both(step + 1, merge_half)
-        both(step + 2, merge_across)
+        each(step + 1, merge_half)
+        each(step + 2, merge_across)
 
     total[...] = selfs[...]
     twin_tile(0).wait_recv()
@@ -554,13 +564,13 @@
         tree = (at.column(-hop) < x).astype(jnp.int32)
         total[tree] += r_in[hop].astype(f32)
 
-    def take(source, way):
+    def take(source):
         z_arrival(source).wait_recv()
         tree = (source < z).astype(jnp.int32)
         total[tree] += z_in[source].astype(f32)
 
-    for step in range(layers - 1, 0, -1):
-        both(step, take)
+    for step in range(reach, 0, -1):
+        each(step, take)
 
     final[...] = total[...].astype(bf16)
 
@@ -593,15 +603,15 @@
     for hop in (1, 3, 2):
         row_copy(hop).wait_send()
 
-    def drain(source, way):
+    def drain(source):
         twin_row(source).wait_send()
         for step in (1, -1):
             x_half(source, step).wait_send()
             x_copy(source, step).wait_send()
-        z_home(source, way).wait_send()
-
-    for step in range(1, layers):
-        both(step, drain)
+        z_home(source).wait_send()
+
+    for step in range(1, layers // 2 + 1):
+        each(step, drain)
 
 
 def scatter_tiles(selfs, back, heads, leaves):
@@ -635,7 +645,10 @@
             dma((X_CHIPS,)), dma((X_CHIPS,)),
         ],
         compiler_params=pltpu.CompilerParams(
-            collective_id=1, has_side_effects=True, vmem_limit_bytes=VMEM_LIMIT
+            collective_id=1, has_side_effects=True, vmem_limit_bytes=SCATTER_VMEM
+        ),
+        cost_estimate=pl.CostEstimate(
+            flops=1 << 34, bytes_accessed=8 << 20, transcendentals=0
         ),
         name="scatter_tiles",
     )(selfs, back)

time: 123 us -> 108 us (0.88)
  the two profiles are of different devices: /device:TPU:80 before, /device:TPU:6 now
where the time goes in v3:
time: 108 us
  Pallas kernels  104 us (96%)
  local copies, waits for them, and re-layouts  3.66 us (3%)
    pallas_call x1, Pallas kernels, gather_tiles(): pl.pallas_call(functools.partial(gather_kernel, heads, leaves), out_shape...  46.5 us
    pallas_call x1, Pallas kernels, scatter_tiles(): pl.pallas_call(functools.partial(scatter_kernel, heads, leaves), out_shap...  37.5 us
    pallas_call x1, Pallas kernels, attend(): pl.pallas_call(attend_kernel, out_shape=(jax.ShapeDtypeStruct(queries.sha...  19.7 us
    unnamed x14, local copies, waits for them, and re-layouts  3.66 us

profile of v3, /device:TPU:6, one launch (start us, length us, event | category | flops | bytes accessed | tf_op | source)
XLA Modules:
  0.0 108.1 jit_solution(8396777702107129197)
XLA Ops:
  0.6 0.0 copy-start.1
  0.6 0.0 copy-start.2
  0.7 0.9 copy-done.2
  1.5 0.0 copy-start.3
  1.5 0.8 copy-done.3
  2.4 0.0 copy-start.4
  2.4 0.7 copy-done.4
  3.0 0.0 copy-start
  3.0 0.0 copy-start.5
  3.0 46.5 %gather_tiles.1 = (bf16[2,272,128]{2,1,0:T(8,128)(2,1)S(1)}, bf16[8,4,2,272,128]{4,3,2,1,0:T(8,128)(2,1)S(1)}) custom-call(s32[2]{0:T(128)S(1)} %copy-done.4, bf16[2,16,1024]{2,1,0:T(8,128)(2,1)S(1)} %copy-done.2, bf16[2,16,1024]{2,1,0:T(8,128)(2,1)S(1)} %copy-done.3), custom_call_target="tpu_custom_call" | custom-call | flops 17179869184 | bytes 8388608 | tf_op jit(solution)/shard_map/gather_tiles/pallas_call | solution.py:238
  49.5 0.0 copy-done.1
  49.6 0.0 copy-done
  49.6 0.0 copy-done.5
  49.6 19.7 %attend.1 = (bf16[2,128,1024]{2,1,0:T(8,128)(2,1)}, f32[2,256,128]{2,1,0:T(8,128)S(1)}, bf16[64,256,128]{2,1,0:T(8,128)(2,1)S(1)}) custom-call(s32[2]{0:T(128)S(1)} %copy-done.5, bf16[2,128,1024]{2,1,0:T(8,128)(2,1)S(1)} %copy-done, bf16[2,128,1024]{2,1,0:T(8,128)(2,1)S(1)} %copy-done.1, bf16[2,272,128]{2,1,0:T(8,128)(2,1)S(1)} %get-tuple-element.10.own, ...), custom_call_target="tpu_custom_call" | custom-call | flops 5033164800 | bytes 12582912 | tf_op jit(solution)/shard_map/attend/pallas_call | solution.py:424
  69.3 37.5 %scatter_tiles.1 = (bf16[2,16,1024]{2,1,0:T(8,128)(2,1)S(1)}, bf16[2,16,1024]{2,1,0:T(8,128)(2,1)S(1)}) custom-call(f32[2,256,128]{2,1,0:T(8,128)S(1)} %get-tuple-element.13.selfs, bf16[8,4,2,256,128]{4,3,2,1,0:T(8,128)(2,1)S(1)} %bitcast.3), custom_call_target="tpu_custom_call" | custom-call | flops 17179869184 | bytes 8388608 | tf_op jit(solution)/shard_map/scatter_tiles/pallas_call | solution.py:624
  106.8 0.6 copy.10
  107.5 0.6 copy.11
Async XLA Ops:
  0.6 48.9 %copy-start.1 = (bf16[2,128,1024]{2,1,0:T(8,128)(2,1)S(1)}, bf16[2,128,1024]{2,1,0:T(8,128)(2,1)}, u32[]{:S(2)}) copy-start(bf16[2,128,1024]{2,1,0:T(8,128)(2,1)} %grads.1) | copy-start | bytes 1572868
  0.6 0.9 copy-start.2
  1.5 0.8 copy-start.3
  2.4 0.7 copy-start.4
  3.0 46.5 %copy-start = (bf16[2,128,1024]{2,1,0:T(8,128)(2,1)S(1)}, bf16[2,128,1024]{2,1,0:T(8,128)(2,1)}, u32[]{:S(2)}) copy-start(bf16[2,128,1024]{2,1,0:T(8,128)(2,1)} %queries.1) | copy-start | bytes 1572868
  3.0 46.5 %copy-start.5 = (s32[2]{0:T(128)S(1)}, s32[2]{0:T(128)}, u32[]{:S(2)}) copy-start(s32[2]{0:T(128)} %first.1) | copy-start | bytes 28

commit v4 on v3

--- a/solution.py
+++ b/solution.py
@@ -17,7 +17,7 @@
 
 X_CHIPS = 4
 ROW = 2 * X_CHIPS
-PARENT_ROWS = 16
+PARENT_ROWS = 8
 KV_ROWS = 2 * BLOCK_TOKENS
 TILE_ROWS = KV_ROWS + PARENT_ROWS
 GATHER_VMEM = 10 * 1024 * 1024
@@ -87,7 +87,7 @@
 
 
 def gather_kernel(
-    heads, leaves, parents, keys, values, own, buf,
+    heads, leaves, parents, local, own, buf,
     y_send, y_recv, z_send, z_recv, r_send, r_recv, x_send, x_recv, h_send, h_recv,
     d_send, d_recv, e_send, e_recv,
 ):
@@ -102,9 +102,9 @@
         rows_v = pl.ds(pl.multiple_of(BLOCK_TOKENS + at.y * share, share), share)
         peer = at.head_peer(step)
         return (
-            remote(keys.at[:, :, column], own.at[:, rows_k, :],
+            remote(local.at[:, pl.ds(0, share), column], own.at[:, rows_k, :],
                    y_send.at[2 * step], y_recv.at[2 * step], peer),
-            remote(values.at[:, :, column], own.at[:, rows_v, :],
+            remote(local.at[:, pl.ds(share, share), column], own.at[:, rows_v, :],
                    y_send.at[2 * step + 1], y_recv.at[2 * step + 1], peer),
         )
 
@@ -112,8 +112,10 @@
         for copy in regroup(step):
             copy.start()
     mine = pl.ds(pl.multiple_of(at.y * HEAD_DIM, HEAD_DIM), HEAD_DIM)
-    own[:, pl.ds(pl.multiple_of(at.y * share, share), share), :] = keys[:, :, mine]
-    own[:, pl.ds(pl.multiple_of(BLOCK_TOKENS + at.y * share, share), share), :] = values[:, :, mine]
+    own[:, pl.ds(pl.multiple_of(at.y * share, share), share), :] = local[:, :share, mine]
+    own[:, pl.ds(pl.multiple_of(BLOCK_TOKENS + at.y * share, share), share), :] = local[
+        :, share:2 * share, mine
+    ]
     for tree in range(2):
         own[tree, KV_ROWS:, :] = jnp.full(
             (PARENT_ROWS, HEAD_DIM), parents[tree].astype(jnp.float32), jnp.float32
@@ -231,7 +233,7 @@
         each(step, drain)
 
 
-def gather_tiles(parents, keys, values, heads, leaves):
+def gather_tiles(parents, local, heads, leaves):
     layers = leaves // ROW
     dma = pltpu.SemaphoreType.DMA
     vmem = pl.BlockSpec(memory_space=pltpu.VMEM)
@@ -241,7 +243,7 @@
             jax.ShapeDtypeStruct((2, TILE_ROWS, HEAD_DIM), jnp.bfloat16),
             jax.ShapeDtypeStruct((layers, X_CHIPS, 2, TILE_ROWS, HEAD_DIM), jnp.bfloat16),
         ),
-        in_specs=[pl.BlockSpec(memory_space=pltpu.SMEM), vmem, vmem],
+        in_specs=[pl.BlockSpec(memory_space=pltpu.SMEM), vmem],
         out_specs=(vmem, vmem),
         scratch_shapes=[
             dma((2 * heads,)), dma((2 * heads,)),
@@ -259,13 +261,14 @@
             flops=1 << 34, bytes_accessed=8 << 20, transcendentals=0
         ),
         name="gather_tiles",
-    )(parents, keys, values)
+    )(parents, local)
 
 
 LANES = 2 * BLOCK_TOKENS
 SPAN = CHAIN * BLOCK_TOKENS
-PART = 3 * BLOCK_TOKENS
+PART = CHAIN * BLOCK_TOKENS
 PARTS = SPAN // PART
+GROUP = 5
 
 
 def attend_kernel(
@@ -328,17 +331,25 @@
         def place_of(link):
             return slice(link * BLOCK_TOKENS, (link + 1) * BLOCK_TOKENS)
 
-        def score_block(pair, link, peak):
-            place, lanes, turn = place_of(link), lanes_of(pair), pair % 2
-            raw = lax.dot_general(kcat[place], q2[lanes], nt, preferred_element_type=jnp.float32)
-            if link == 0:
-                raw = jnp.where(causal, raw, masked_score)
-            s_scr[turn, place] = raw
+        def score_group(pair, group, peak):
+            lanes, turn = lanes_of(pair), pair % 2
+            place = slice(group * GROUP * BLOCK_TOKENS, (group + 1) * GROUP * BLOCK_TOKENS)
+            s_scr[turn, place] = lax.dot_general(
+                kcat[place], q2[lanes], nt, preferred_element_type=jnp.float32
+            )
             l_scr[turn, place] = lax.dot_general(
                 vcat[place], g2[lanes], nt, preferred_element_type=jnp.float32
             )
-            top = jnp.max(raw.reshape(-1, 8, LANES), 0) * log2_scale + bias[link]
-            return top if peak is None else jnp.maximum(peak, top)
+            for link in range(group * GROUP, (group + 1) * GROUP):
+                here = place_of(link)
+                if link == 0:
+                    s_scr[turn, here] = jnp.where(causal, s_scr[turn, here], masked_score)
+                top = s_scr[turn, here.start:here.start + 16]
+                for row in range(here.start + 16, here.stop, 16):
+                    top = jnp.maximum(top, s_scr[turn, row:row + 16])
+                top = top * log2_scale + bias[link]
+                peak = top if peak is None else jnp.maximum(peak, top)
+            return peak
 
         def sum_block(pair, link, peak, total, lean):
             turn = pair % 2
@@ -370,24 +381,24 @@
 
         pairs = rows // LANES
         peak = None
-        for link in range(CHAIN):
-            peak = score_block(0, link, peak)
+        groups = CHAIN // GROUP
+        for group in range(groups):
+            peak = score_group(0, group, peak)
         for pair in range(pairs):
             peak = jnp.max(peak, 0, keepdims=True)
             total = jnp.zeros((16, LANES), jnp.float32)
             lean = jnp.zeros((16, LANES), jnp.float32)
             later = None
-            half = (CHAIN + 1) // 2
+            done = 0
             for link in range(CHAIN):
                 total, lean = sum_block(pair, link, peak, total, lean)
-                if pair + 1 < pairs and link % 2 == 0:
-                    later = score_block(pair + 1, link // 2, later)
+                if pair + 1 < pairs and done < groups and 2 * done * CHAIN <= link * 2 * groups:
+                    later = score_group(pair + 1, done, later)
+                    done += 1
             inverse = 1.0 / jnp.sum(total, 0, keepdims=True)
             mean = jnp.sum(lean, 0, keepdims=True) * inverse
             for link in range(CHAIN):
                 weight_block(pair, link, inverse, mean)
-                if pair + 1 < pairs and link % 2 == 1:
-                    later = score_block(pair + 1, half + link // 2, later)
             query_part(pair)
             peak = later
 
@@ -656,7 +667,8 @@
 
 def body(queries, keys, values, output_gradient, parents):
     heads, leaves = lax.axis_size("head"), lax.axis_size("leaf")
-    own, buf = gather_tiles(parents, keys, values, heads, leaves)
+    local = jnp.concatenate([keys, values], axis=1)
+    own, buf = gather_tiles(parents, local, heads, leaves)
     buf = buf.reshape(leaves, TILE_ROWS, HEAD_DIM)
     query_grads, selfs, back = attend(parents, queries, output_gradient, own, buf)
     back = back.reshape(leaves // ROW, X_CHIPS, 2, KV_ROWS, HEAD_DIM)

time: 108 us -> 105 us (0.972)
  Pallas kernels: 104 us -> 101 us
  local copies, waits for them, and re-layouts: 3.66 us -> 1.92 us
    pallas_call x1, Pallas kernels: 19.7 us -> 17.5 us  [attend(): pl.pallas_call(attend_kernel, out_shape=(jax.ShapeDtypeStruct(queries.sha...]
    unnamed x14 -> x10, local copies, waits for them, and re-layouts: 3.66 us -> 1.92 us
where the time goes in v4:
time: 105 us
  Pallas kernels  101 us (96%)
  local copies, waits for them, and re-layouts  1.92 us (2%)
    pallas_call x1, Pallas kernels, gather_tiles(): pl.pallas_call(functools.partial(gather_kernel, heads, leaves), out_shape...  45.8 us
    pallas_call x1, Pallas kernels, scatter_tiles(): pl.pallas_call(functools.partial(scatter_kernel, heads, leaves), out_shap...  37.8 us
    pallas_call x1, Pallas kernels, attend(): pl.pallas_call(attend_kernel, out_shape=(jax.ShapeDtypeStruct(queries.sha...  17.5 us

profile of v4, /device:TPU:6, one launch (start us, length us, event | category | flops | bytes accessed | tf_op | source)
XLA Modules:
  0.0 104.6 jit_solution(13777274572868667990)
XLA Ops:
  0.6 0.9 pad_maximum_fusion.local
  1.5 0.0 copy-start.2
  1.5 0.6 copy-done.2
  2.2 0.0 copy-start
  2.2 0.0 copy-start.1
  2.2 0.0 copy-start.3
  2.2 45.8 %gather_tiles.1 = (bf16[2,264,128]{2,1,0:T(8,128)(2,1)S(1)}, bf16[8,4,2,264,128]{4,3,2,1,0:T(8,128)(2,1)S(1)}) custom-call(s32[2]{0:T(128)S(1)} %copy-done.2, bf16[2,32,1024]{2,1,0:T(8,128)(2,1)S(1)} %pad_maximum_fusion.local), custom_call_target="tpu_custom_call" | custom-call | flops 17179869184 | bytes 8388608 | tf_op jit(solution)/shard_map/gather_tiles/pallas_call | solution.py:240
  48.0 0.0 copy-done
  48.0 0.0 copy-done.1
  48.0 0.0 copy-done.3
  48.0 17.5 %attend.1 = (bf16[2,128,1024]{2,1,0:T(8,128)(2,1)}, f32[2,256,128]{2,1,0:T(8,128)S(1)}, bf16[64,256,128]{2,1,0:T(8,128)(2,1)S(1)}) custom-call(s32[2]{0:T(128)S(1)} %copy-done.3, bf16[2,128,1024]{2,1,0:T(8,128)(2,1)S(1)} %copy-done, bf16[2,128,1024]{2,1,0:T(8,128)(2,1)S(1)} %copy-done.1, bf16[2,264,128]{2,1,0:T(8,128)(2,1)S(1)} %get-tuple-element.10.own, ...), custom_call_target="tpu_custom_call" | custom-call | flops 5033164800 | bytes 12582912 | tf_op jit(solution)/shard_map/attend/pallas_call | solution.py:435
  65.5 37.8 %scatter_tiles.1 = (bf16[2,16,1024]{2,1,0:T(8,128)(2,1)S(1)}, bf16[2,16,1024]{2,1,0:T(8,128)(2,1)S(1)}) custom-call(f32[2,256,128]{2,1,0:T(8,128)S(1)} %get-tuple-element.13.selfs, bf16[8,4,2,256,128]{4,3,2,1,0:T(8,128)(2,1)S(1)} %bitcast.3), custom_call_target="tpu_custom_call" | custom-call | flops 17179869184 | bytes 8388608 | tf_op jit(solution)/shard_map/scatter_tiles/pallas_call | solution.py:635
  103.3 0.6 copy.10
  103.9 0.6 copy.11
Async XLA Ops:
  1.5 0.7 copy-start.2
  2.2 45.8 %copy-start = (bf16[2,128,1024]{2,1,0:T(8,128)(2,1)S(1)}, bf16[2,128,1024]{2,1,0:T(8,128)(2,1)}, u32[]{:S(2)}) copy-start(bf16[2,128,1024]{2,1,0:T(8,128)(2,1)} %queries.1) | copy-start | bytes 1572868
  2.2 45.8 %copy-start.1 = (bf16[2,128,1024]{2,1,0:T(8,128)(2,1)S(1)}, bf16[2,128,1024]{2,1,0:T(8,128)(2,1)}, u32[]{:S(2)}) copy-start(bf16[2,128,1024]{2,1,0:T(8,128)(2,1)} %grads.1) | copy-start | bytes 1572868
  2.2 45.8 %copy-start.3 = (s32[2]{0:T(128)S(1)}, s32[2]{0:T(128)}, u32[]{:S(2)}) copy-start(s32[2]{0:T(128)} %first.1) | copy-start | bytes 28
